TPU v7x, 32 devices: a whole 2x2x4 slice. The times are simulated.
32 devices in a mesh: gx: 8 (over z, y), gy: 4 (over x, core).
Axes of the slice: x: 2, y: 2, z: 4, core: 2. Of those that a mesh axis runs over, the one named last changes fastest.
Arguments:
- modes: float32 [2, 3, 96, 64, 128], P(None, None, 'gx', 'gy'), may hold values from -6 to 6
- moduli: float32 [96, 64, 128], P('gx', 'gy'), may hold values from 0.5 to 2
- pinned: int32 [96, 64, 128], P('gx', 'gy'), may hold values 0 or 1
- spectrum: float32 [3, 2], replicated, may hold values from 0.175 to 5, as said below
Outputs:
- correction: float32 [2, 3, 96, 64, 128], P(None, None, 'gx', 'gy')
Inputs may be any that keep to these rules, and one draw needn't show every extreme that they name: spectrum[l] = (lower, upper) with upper from 3.5 to 5 and lower 0.05 to 0.15 times upper.
All inputs are finite; a program needn't handle non-finite values. No bound on the sum of `pinned` on one device may be relied on, other than what follows from the above.
Results may differ from a plain program's by a relative error of at most 0.0003.
Values sent between devices are 32-bit elements; how exact they have to be, the bound alone decides.
A program may use at most 128 MiB of HBM per device.

v0:
```python
import functools

import jax
import jax.numpy as jnp
import numpy as np
from jax import lax
from jax.experimental import pallas as pl
from jax.experimental.pallas import tpu as pltpu
from jax.sharding import PartitionSpec as P

DEG = 3
COARSE_DEG = 4
DEGREES = (4, 2, 1)
MU_SHEAR = 1.0
LAMBDA_BULK = 1.5
PROLONG_TABLES = {
    4: np.array(
        [[1.0, 0.0, 0.0], [0.375, 0.75, -0.125], [0.0, 1.0, 0.0], [-0.125, 0.75, 0.375]]
    ),
    2: np.array([[1.0, 0.0], [0.5, 0.5]]),
}
DIRS = ((-1, 0), (0, -1), (1, 0), (0, 1), (-1, -1), (-1, 1), (1, -1), (1, 1))
F32 = jnp.float32
BF16 = jnp.bfloat16


def assemble(element, degree):
    table = np.zeros((degree, 2 * degree + 1))
    for residue in range(degree):
        for offset in range(-degree, degree + 1):
            target = residue + offset
            if 0 <= target <= degree:
                table[residue, offset + degree] += element[residue, target]
            if residue == 0 and offset <= 0:
                table[residue, offset + degree] += element[degree, degree + offset]
    return table


def basis_tables(degree):
    nodes = [float(place) / degree for place in range(degree + 1)]
    gauss_x, gauss_w = np.polynomial.legendre.leggauss(8)
    points = 0.5 * (gauss_x + 1.0)
    weights = 0.5 * gauss_w
    values = np.zeros((degree + 1, points.size))
    slopes = np.zeros((degree + 1, points.size))
    for column in range(degree + 1):
        product = np.ones(points.size)
        for other in range(degree + 1):
            if other != column:
                product = product * (points - nodes[other]) / (nodes[column] - nodes[other])
        values[column] = product
        for skipped in range(degree + 1):
            if skipped != column:
                part = np.ones(points.size) / (nodes[column] - nodes[skipped])
                for other in range(degree + 1):
                    if other != column and other != skipped:
                        part = part * (points - nodes[other]) / (nodes[column] - nodes[other])
                slopes[column] += part
    mass = (values * weights) @ values.T
    stiff = (slopes * weights) @ slopes.T
    mixed = (slopes * weights) @ values.T
    return [assemble(e, degree) for e in (mass, stiff, mixed, mixed.T)]


def dense(table, count):
    p = table.shape[0]
    out = np.zeros((count, count + p + 1))
    for i in range(count):
        for o in range(-p, p + 1):
            c = table[i % p, o + p]
            if c != 0.0 and i + o <= count:
                out[i, i + o + p] += c
    return out


def up8(n):
    return -(-n // 8) * 8


class Level:
    def __init__(self, degree, nx, ny, nz, vecs):
        p = self.p = degree
        self.nx, self.ny, self.nz, self.vecs = nx, ny, nz, vecs
        self.own = nx * ny
        self.rows = up8(self.own)
        self.lanes = -(-vecs * nz // 128) * 128
        self.blocked = nz % 128 == 0
        self.pos = [(x, y) for x in range(nx) for y in range(ny)]
        self.pos += [None] * (self.rows - self.own)
        self.blocks = []
        self.halo_pos = []
        for dx, dy in DIRS:
            src_x = {-1: range(nx - p, nx), 0: range(nx), 1: range(1)}[dx]
            src_y = {-1: range(ny - p, ny), 0: range(ny), 1: range(1)}[dy]
            start = len(self.halo_pos)
            runs = []
            for x in src_x:
                at = len(self.halo_pos)
                runs.append((at, x * ny + src_y[0], len(src_y)))
                self.halo_pos += [(x + dx * nx, y + dy * ny) for y in src_y]
            merged = [runs[0]]
            for run in runs[1:]:
                a, b, n = merged[-1]
                if run[0] == a + n and run[1] == b + n:
                    merged[-1] = (a, b, n + run[2])
                else:
                    merged.append(run)
            size = up8(len(self.halo_pos) - start)
            self.halo_pos += [None] * (start + size - len(self.halo_pos))
            self.blocks.append((start, size, merged))
        self.halo = len(self.halo_pos)

    def plane(self, mat_x, mat_y, rows_out, positions):
        out = np.zeros((rows_out, len(positions)))
        for k, at in enumerate(positions):
            if at is not None:
                col = np.outer(mat_x[:, at[0] + self.p], mat_y[:, at[1] + self.p]).ravel()
                out[: col.size, k] = col
        return out

    def operator(self):
        t = basis_tables(self.p)
        m_x, k_x, g_x, t_x = [dense(e, self.nx) for e in t]
        m_y, k_y, g_y, t_y = [dense(e, self.ny) for e in t]
        cc = LAMBDA_BULK + MU_SHEAR
        big = MU_SHEAR + cc
        groups = [
            [((big, k_x, m_y), (MU_SHEAR, m_x, k_y)), ((1, m_x, m_y),), ((cc, t_x, g_y),), ((cc, t_x, m_y),)],
            [((MU_SHEAR, k_x, m_y), (big, m_x, k_y)), ((1, m_x, m_y),), ((cc, g_x, t_y),), ((cc, m_x, t_y),)],
            [((MU_SHEAR, k_x, m_y), (MU_SHEAR, m_x, k_y)), ((1, m_x, m_y),), ((cc, g_x, m_y),), ((cc, m_x, g_y),)],
        ]

        def build(positions):
            return np.stack(
                [
                    np.concatenate(
                        [
                            sum(w * self.plane(a, b, self.rows, positions) for w, a, b in terms)
                            for terms in source
                        ]
                    )
                    for source in groups
                ]
            )

        line = [dense(e, self.nz)[:, self.p : self.p + self.nz] for e in t]
        line = [e.T if self.blocked else self.lift_z(e, self) for e in line]
        z_ops = np.stack([line[0], MU_SHEAR * line[1], big * line[1], line[2], line[3]])
        return build(self.pos), build(self.halo_pos), z_ops

    def lift_z(self, mat, to):
        full = np.kron(np.eye(self.vecs), mat.T)
        out = np.zeros((self.lanes, to.lanes))
        out[: full.shape[0], : full.shape[1]] = full
        return out

    def diagonal(self):
        t = basis_tables(self.p)

        def center(table, count):
            return table[np.arange(count) % self.p, self.p]

        m_x, m_y, m_z = [center(t[0], n) for n in (self.nx, self.ny, self.nz)]
        k_x, k_y, k_z = [center(t[1], n) for n in (self.nx, self.ny, self.nz)]
        rows = np.zeros((self.rows, 128), np.float32)
        for c in range(3):
            coef = [MU_SHEAR + (LAMBDA_BULK + MU_SHEAR) * (c == e) for e in range(3)]
            plane = coef[0] * np.outer(k_x, m_y) + coef[1] * np.outer(m_x, k_y)
            rows[: self.own, c] = plane.ravel()
            rows[: self.own, 3 + c] = (coef[2] * np.outer(m_x, m_y)).ravel()
        lanes = np.zeros((8, self.lanes), np.float32)
        lanes[0, : self.vecs * self.nz] = np.tile(m_z, self.vecs)
        lanes[1, : self.vecs * self.nz] = np.tile(k_z, self.vecs)
        return rows, lanes

    def sample(self, top):
        step = top.p // self.p
        sel_x = np.zeros((self.rows, top.own))
        for i, (x, y) in enumerate(self.pos[: self.own]):
            sel_x[i, x * step * top.ny + y * step] = 1
        sel_z = np.zeros((top.nz, self.lanes))
        for v in range(self.vecs):
            for z in range(self.nz):
                sel_z[z * step, v * self.nz + z] = 1
        return sel_x, sel_z


def prolong_dense(table, fine_n, lead):
    q = table.shape[0]
    half = q // 2
    out = np.zeros((fine_n, fine_n // 2 + lead + 1))
    for i in range(fine_n):
        for t in range(half + 1):
            j = half * (i // q) + t
            out[i, j + lead] += table[i % q, t]
    return out


def restrict_dense(table, fine_n):
    q = table.shape[0]
    half = q // 2
    out = np.zeros((fine_n // 2, fine_n + q + 1))
    for j in range(fine_n // 2):
        for i in range(-q, fine_n):
            t = j - half * (i // q)
            if 0 <= t <= half:
                out[j, i + q] += table[i % q, t]
    return out


def transfer(fine, coarse):
    table = PROLONG_TABLES[fine.p]
    rx, ry = restrict_dense(table, fine.nx), restrict_dense(table, fine.ny)
    rz = restrict_dense(table, fine.nz)[:, fine.p : fine.p + fine.nz]
    px = prolong_dense(table, fine.nx, coarse.p)
    py = prolong_dense(table, fine.ny, coarse.p)
    pz = prolong_dense(table, fine.nz, coarse.p)[:, coarse.p : coarse.p + coarse.nz]
    return (
        fine.plane(rx, ry, coarse.rows, fine.pos),
        fine.plane(rx, ry, coarse.rows, fine.halo_pos),
        fine.lift_z(rz, coarse),
        coarse.plane(px, py, fine.rows, coarse.pos),
        coarse.plane(px, py, fine.rows, coarse.halo_pos),
        coarse.lift_z(pz, fine),
    )


def split(mat):
    mat = np.asarray(mat, np.float32)
    hi = mat.astype(BF16)
    return [hi, (mat - hi.astype(np.float32)).astype(BF16)]


def halves(value):
    hi = value.astype(BF16)
    return hi, (value - hi.astype(F32)).astype(BF16)


def dot3(a, b):
    def one(u, v):
        return lax.dot_general(u, v, (((1,), (0,)), ((), ())), preferred_element_type=F32)

    return one(a[0], b[0]) + one(a[0], b[1]) + one(a[1], b[0])


def kernel(levels, names, *refs):
    R = dict(zip(names, refs))
    gx_n, gy_n = lax.axis_size("gx"), lax.axis_size("gy")
    me_x, me_y = lax.axis_index("gx"), lax.axis_index("gy")

    def reach(dx, dy):
        ok = None
        for d, me, n in ((dx, me_x, gx_n), (dy, me_y, gy_n)):
            if d:
                here = me + d < n if d > 0 else me + d >= 0
                ok = here if ok is None else jnp.logical_and(ok, here)
        return ok

    def device(dx, dy):
        return (jnp.clip(me_x + dx, 0, gx_n - 1), jnp.clip(me_y + dy, 0, gy_n - 1))

    top = levels[0]
    vecs, nz = top.vecs, top.nz
    if top.blocked:
        for h in "hl":
            R[f"z0{h}"][...] = jnp.zeros_like(R[f"z0{h}"])
    moves = [(R["moduli_in"], R["moduli"]), (R["pinned_in"], R["pinned"])]
    for v in range(vecs):
        moves.append((R["modes"].at[v], R["r0"].at[:, :, pl.ds(v * nz, nz)]))
    for name in names:
        if name.endswith("_in") and name[:-3] not in ("moduli", "pinned"):
            src, dst = R[name], R[name[:-3]]
            if name[:2] == "z0" and top.blocked:
                for v in range(vecs):
                    at = pl.ds(v * nz, nz)
                    moves.append((src, dst.at[:, at, at]))
            else:
                moves.append((src, dst))
    moves = [
        pltpu.make_async_copy(src, dst, R["lsem"].at[i]) for i, (src, dst) in enumerate(moves)
    ]
    for one in moves:
        one.start()
    chebyshev_table(R["spectrum"], R["coef"])
    for l, lev in enumerate(levels):
        R[f"halo{l}"][...] = jnp.zeros_like(R[f"halo{l}"])
        R[f"send{l}"][...] = jnp.zeros_like(R[f"send{l}"])
    barrier = pltpu.get_barrier_semaphore()
    for dx, dy in DIRS:

        @pl.when(reach(dx, dy))
        def _():
            pl.semaphore_signal(
                barrier, inc=1, device_id=device(dx, dy), device_id_type=pl.DeviceIdType.MESH
            )

    around = [
        1 + (me > 0).astype(jnp.int32) + (me < n - 1).astype(jnp.int32)
        for me, n in ((me_x, gx_n), (me_y, gy_n))
    ]
    pl.semaphore_wait(barrier, around[0] * around[1] - 1)

    def copies(l, slot, side):
        for i, (dx, dy) in enumerate(DIRS):
            if side and -side in (dx, dy):
                continue
            start, size, _ = levels[l].blocks[i]
            yield (
                dx,
                dy,
                pltpu.make_async_remote_copy(
                    src_ref=R[f"send{l}"].at[:, pl.ds(start, size), :],
                    dst_ref=R[f"halo{l}"].at[slot, :, pl.ds(start, size), :],
                    send_sem=R[f"ssem{l}"].at[i],
                    recv_sem=R[f"rsem{l}"].at[slot, i],
                    device_id=device(-dx, -dy),
                    device_id_type=pl.DeviceIdType.MESH,
                ),
            )

    def exchange(l, slot, value, side=0):
        lev = levels[l]
        work, send = R[f"work{l}"], R[f"send{l}"]

        def stage(c, _):
            work[c] = value(c)
            for _, _, runs in lev.blocks:
                for at, src, n in runs:
                    send[c, at : at + n, :] = work[c, src : src + n, :]
            return 0

        lax.fori_loop(0, 3, stage, 0)
        for dx, dy, copy in copies(l, slot, side):
            pl.when(reach(-dx, -dy))(copy.start)

    def arrive(l, slot, side=0):
        for dx, dy, copy in copies(l, slot, side):
            pl.when(reach(dx, dy))(copy.wait_recv)
            pl.when(reach(-dx, -dy))(copy.wait_send)

    def pair(name, *at):
        return tuple(R[name + h][at] if at else R[name + h][...] for h in ("h", "l"))

    def apply_step(l, k, slot):
        lev = levels[l]
        rows = lev.rows
        s, d, r, x, prod = (R[f"{n}{l}"] for n in ("s", "d", "r", "x", "prod"))
        exchange(l, slot, lambda c: s[...] * d[c])

        def near(c, _):
            prod[c] = dot3(pair(f"wo{l}", c), halves(R[f"work{l}"][c]))
            return 0

        def far(c, _):
            prod[c] += dot3(pair(f"wh{l}", c), halves(R[f"halo{l}"][slot, c]))
            return 0

        lax.fori_loop(0, 3, near, 0)
        arrive(l, slot)
        lax.fori_loop(0, 3, far, 0)

        def group(c, g):
            return prod[c, g * rows : (g + 1) * rows, :]

        zmat = [pair(f"z{l}", i) for i in range(5)]
        parts = [
            ((group(0, 0) + group(1, 2), 0), (group(0, 1), 1), (group(2, 2), 4)),
            ((group(1, 0) + group(0, 2), 0), (group(1, 1), 1), (group(2, 3), 4)),
            ((group(2, 0), 0), (group(2, 1), 2), (group(0, 3) + group(1, 3), 3)),
        ]
        c1 = R["coef"][l, 2 * k]
        c2 = R["coef"][l, 2 * k + 1]
        for c in range(3):
            total = None
            for val, z in parts[c]:
                one = dot3(halves(val), zmat[z])
                total = one if total is None else total + one
            res = r[c] - (s[...] * total + R[f"f{l}"][...] * d[c])
            r[c] = res
            new = c1 * d[c] + c2 * (R[f"dinv{l}"][c] * res)
            d[c] = new
            x[c] += new

    def move(l, slot, value, name, out, side):
        exchange(l, slot, value, side)
        arrive(l, slot, side)

        def one(c, _):
            flat = dot3(pair(name + "o"), halves(R[f"work{l}"][c]))
            flat += dot3(pair(name + "h"), halves(R[f"halo{l}"][slot, c]))
            out(c, dot3(halves(flat), pair(name + "z")))
            return 0

        lax.fori_loop(0, 3, one, 0)

    def start(l, c, b):
        first = R["coef"][l, 12] * (R[f"dinv{l}"][c] * b)
        R[f"r{l}"][c] = b
        R[f"d{l}"][c] = first
        R[f"x{l}"][c] = first

    def run(l):
        last = l == len(levels) - 1

        def body(k, _):
            slot = k % 2 if last else (k + k // 3) % 2
            apply_step(l, k, slot)
            if not last:

                @pl.when(k == DEG - 1)
                def _():
                    def down(c, val):
                        start(l + 1, c, (1.0 - R[f"f{l + 1}"][...]) * val)

                    def up(c, val):
                        step = (1.0 - R[f"f{l}"][...]) * val
                        R[f"d{l}"][c] = step
                        R[f"x{l}"][c] += step

                    move(l, 1, lambda c: (1.0 - R[f"f{l}"][...]) * R[f"r{l}"][c], f"rs{l}", down, -1)
                    run(l + 1)
                    move(l + 1, 1, lambda c: R[f"x{l + 1}"][c], f"pr{l}", up, 1)

            return 0

        lax.fori_loop(0, COARSE_DEG - 1 if last else 2 * DEG, body, 0)

    for one in moves:
        one.wait()
    free = 1.0 - R["pinned"][...].astype(F32)
    scale = R["moduli"][...] * free

    def times01(a, b):
        return lax.dot_general(a, b, (((1,), (0,)), ((), ())), preferred_element_type=F32)

    def thirds(value):
        hi, lo = halves(value)
        rest = value - hi.astype(F32) - lo.astype(F32)
        return hi, lo, rest.astype(BF16)

    for l, lev in enumerate(levels):
        if l == 0 and lev.blocked:
            for v in range(vecs):
                at = pl.ds(v * nz, nz)
                R["s0"][:, at] = scale
                R["f0"][:, at] = 1.0 - free
        else:
            sel_x, sel_z = R[f"sx{l}"][...], R[f"sz{l}"][...]
            picked = sum(times01(sel_x, part) for part in thirds(scale))
            R[f"s{l}"][...] = sum(times01(part, sel_z) for part in thirds(picked))
            picked = times01(sel_x, free.astype(BF16))
            R[f"f{l}"][...] = 1.0 - times01(picked.astype(BF16), sel_z)
        square = R[f"s{l}"][...] * R[f"s{l}"][...]
        m_z, k_z = R[f"kl{l}"][0:1, :], R[f"kl{l}"][1:2, :]
        for c in range(3):
            kd = R[f"kr{l}"][:, c : c + 1] * m_z + R[f"kr{l}"][:, 3 + c : 4 + c] * k_z
            R[f"dinv{l}"][c] = 1.0 / (square * kd + R[f"f{l}"][...])
    for c in range(3):
        start(0, c, R["r0"][c])
    run(0)
    backs = [
        pltpu.make_async_copy(
            R["x0"].at[:, :, pl.ds(v * nz, nz)], R["out"].at[v], R["lsem"].at[v]
        )
        for v in range(vecs)
    ]
    for one in backs:
        one.start()
    for one in backs:
        one.wait()


def chebyshev_table(spectrum, coef):
    for l in range(3):
        low, top = spectrum[l, 0], spectrum[l, 1]
        center = 0.5 * (top + low)
        radius = 0.5 * (top - low)
        ratio = center / radius
        rho = 1.0 / ratio
        steps = []
        for _ in range(COARSE_DEG - 1):
            rho_next = 1.0 / (2.0 * ratio - rho)
            steps.append((rho_next * rho, 2.0 * rho_next / radius))
            rho = rho_next
        smooth = steps[: DEG - 1]
        flat = [(0.0, 0.0), (0.0, 1.0 / center)]
        picked = steps if l == 2 else smooth + flat + smooth
        for k, two in enumerate(picked):
            coef[l, 2 * k] = jnp.asarray(two[0], F32)
            coef[l, 2 * k + 1] = jnp.asarray(two[1], F32)
        coef[l, 12] = 1.0 / center


def local(modes, moduli, pinned, spectrum):
    vecs, _, nx, ny, nz = modes.shape
    levels = []
    names, args = [], []

    def add(name, value):
        names.append(name)
        args.append(value)

    for l, degree in enumerate(DEGREES):
        step = DEGREES[0] // degree
        levels.append(Level(degree, nx // step, ny // step, nz // step, vecs))
    add("spectrum", spectrum)
    add("modes", modes.reshape(vecs, 3, nx * ny, nz))
    add("moduli_in", moduli.reshape(nx * ny, nz))
    add("pinned_in", pinned.reshape(nx * ny, nz))
    for l, lev in enumerate(levels):
        mats = dict(zip((f"wo{l}", f"wh{l}", f"z{l}"), lev.operator()))
        if l + 1 < len(levels):
            keys = [f"{a}{l}{b}" for a in ("rs", "pr") for b in "ohz"]
            mats.update(zip(keys, transfer(lev, levels[l + 1])))
        for key, mat in mats.items():
            for tag, half in zip("hl", split(mat)):
                add(key + tag + "_in", jnp.asarray(half))
        for key, mat in zip(("kr", "kl"), lev.diagonal()):
            add(f"{key}{l}_in", jnp.asarray(mat))
        if l or not lev.blocked:
            for key, mat in zip(("sx", "sz"), lev.sample(levels[0])):
                add(f"{key}{l}_in", jnp.asarray(mat.astype(BF16)))

    specs = [
        pl.BlockSpec(memory_space=pltpu.SMEM if n == "spectrum" else pl.ANY) for n in names
    ]
    scratch = []
    all_names = names + ["out"]

    def temp(name, what):
        all_names.append(name)
        scratch.append(what)

    temp("coef", pltpu.SMEM((3, 13), F32))
    temp("lsem", pltpu.SemaphoreType.DMA((len(names) + 2 * vecs,)))
    for name, value in zip(names, args):
        if name.endswith("_in"):
            shape = value.shape
            if name[:2] == "z0" and levels[0].blocked:
                shape = (shape[0], levels[0].lanes, levels[0].lanes)
            temp(name[:-3], pltpu.VMEM(shape, value.dtype))
    for l, lev in enumerate(levels):
        field = (3, lev.rows, lev.lanes)
        for n in ("s", "f"):
            temp(f"{n}{l}", pltpu.VMEM(field[1:], F32))
        for n in ("r", "d", "x", "work", "dinv"):
            temp(f"{n}{l}", pltpu.VMEM(field, F32))
        temp(f"prod{l}", pltpu.VMEM((3, 4 * lev.rows, lev.lanes), F32))
        temp(f"send{l}", pltpu.VMEM((3, lev.halo, lev.lanes), F32))
        temp(f"halo{l}", pltpu.VMEM((2, 3, lev.halo, lev.lanes), F32))
        temp(f"ssem{l}", pltpu.SemaphoreType.DMA((len(DIRS),)))
        temp(f"rsem{l}", pltpu.SemaphoreType.DMA((2, len(DIRS))))
    out = pl.pallas_call(
        functools.partial(kernel, levels, all_names),
        out_shape=jax.ShapeDtypeStruct((vecs, 3, nx * ny, nz), F32),
        in_specs=specs,
        out_specs=pl.BlockSpec(memory_space=pl.ANY),
        scratch_shapes=scratch,
        compiler_params=pltpu.CompilerParams(
            collective_id=0, has_side_effects=True, vmem_limit_bytes=60 * 1024 * 1024
        ),
    )(*args)
    return out.reshape(modes.shape)


def solution(mesh):
    placed = (P(None, None, "gx", "gy", None), P("gx", "gy", None), P("gx", "gy", None), P())
    return jax.shard_map(
        local,
        mesh=mesh,
        in_specs=placed,
        out_specs=P(None, None, "gx", "gy", None),
        check_vma=False,
    )
```

profile of v0, /device:TPU:17, one launch (start us, length us, event | category | flops | bytes accessed | tf_op | source)
XLA Modules:
  0.0 147.3 jit_solution(14228341605715265744)
XLA Ops:
  0.0 1.3 copy.57.refs_0_
  1.3 0.6 jit_solution_.37.refs_33_
  1.9 0.6 jit_solution_.36.refs_31_
  2.5 0.6 jit_solution_.39.refs_39_
  3.1 0.6 jit_solution_.38.refs_37_
  3.7 0.6 jit_solution_.31.refs_13_
  4.3 0.6 jit_solution_.30.refs_11_
  4.9 0.6 call_exported.0.refs_35_.refs_41_
  5.5 0.6 jit_solution_.34.refs_19_
  6.2 0.6 jit_solution_.33.refs_17_
  6.8 0.6 jit_solution_.35.refs_21_
  7.4 0.6 jit_solution_.32.refs_15_
  8.0 137.3 %shard_map.514 = f32[2,3,192,128]{3,2,1,0:T(8,128)} custom-call(f32[3,2]{1,0:T(4,128)} %copy.57.refs_0_, f32[2,3,192,128]{3,2,1,0:T(8,128)} %bitcast.5, f32[192,128]{1,0:T(8,128)} %bitcast.6, s32[192,128]{1,0:T(8,128)} %bitcast.7, bf16[3,768,192]{2,1,0:T(8,128)(2,1)} %constant.102.clone.refs_4_, bf16[3,768,192]{2,1,0:T(8,128)(2,1)} %constant.103.clone.refs_5_, ...), custom_call_target="tpu_custom_call" | custom-call | tf_op jit(solution)/shard_map/pallas_call | solution.py:553
  145.4 1.9 %copy.59 = f32[2,3,12,16,128]{4,3,2,1,0:T(8,128)} copy(f32[2,3,12,16,128]{4,3,2,1,0:T(8,128)} %bitcast.4) | data formatting | bytes 1179648
where the time goes:
time: 148 us; the launch traced here: 147 us
  Pallas kernels  137 us (93%)
  local copies, waits for them, and re-layouts  9.98 us (7%)
    pallas_call x1, Pallas kernels, local(): pl.pallas_call(functools.partial(kernel, levels, all_names), out_shape=ja...  137 us
    another operation x11, local copies, waits for them, and re-layouts  6.7 us
    unnamed x2, local copies, waits for them, and re-layouts  3.28 us

commit v1 on v0

v1 whole, which is shorter than its diff:
```python
import functools

import jax
import jax.numpy as jnp
import numpy as np
from jax import lax
from jax.experimental import pallas as pl
from jax.experimental.pallas import tpu as pltpu
from jax.sharding import PartitionSpec as P

DEG = 3
COARSE_DEG = 4
DEGREES = (4, 2, 1)
MU_SHEAR = 1.0
LAMBDA_BULK = 1.5
PROLONG_TABLES = {
    4: np.array(
        [[1.0, 0.0, 0.0], [0.375, 0.75, -0.125], [0.0, 1.0, 0.0], [-0.125, 0.75, 0.375]]
    ),
    2: np.array([[1.0, 0.0], [0.5, 0.5]]),
}
DIRS = ((-1, 0), (1, 0), (0, -1), (0, 1), (-1, -1), (-1, 1), (1, -1), (1, 1))
F32 = jnp.float32
BF16 = jnp.bfloat16
M_, K_, G_, T_ = range(4)


def element_matrices(degree):
    nodes = [float(place) / degree for place in range(degree + 1)]
    gauss_x, gauss_w = np.polynomial.legendre.leggauss(8)
    points = 0.5 * (gauss_x + 1.0)
    weights = 0.5 * gauss_w
    values = np.zeros((degree + 1, points.size))
    slopes = np.zeros((degree + 1, points.size))
    for column in range(degree + 1):
        product = np.ones(points.size)
        for other in range(degree + 1):
            if other != column:
                product = product * (points - nodes[other]) / (nodes[column] - nodes[other])
        values[column] = product
        for skipped in range(degree + 1):
            if skipped != column:
                part = np.ones(points.size) / (nodes[column] - nodes[skipped])
                for other in range(degree + 1):
                    if other != column and other != skipped:
                        part = part * (points - nodes[other]) / (nodes[column] - nodes[other])
                slopes[column] += part
    mass = (values * weights) @ values.T
    stiff = (slopes * weights) @ slopes.T
    mixed = (slopes * weights) @ values.T
    return [mass, stiff, mixed, mixed.T]


def assembled(element, count, ghost):
    p = element.shape[0] - 1
    out = np.zeros((count + 1, count + 1))
    for e in range(count // p):
        out[e * p : e * p + p + 1, e * p : e * p + p + 1] += element
    if ghost:
        out[0, 0] += element[p, p]
    return out


def up(n, m):
    return -(-n // m) * m


def bf16_parts(mat, count):
    rest = np.asarray(mat, np.float64)
    parts = []
    for _ in range(count):
        part = rest.astype(np.float32).astype(BF16)
        parts.append(part)
        rest = rest - part.astype(np.float64)
    return parts


def exact_bf16(mat):
    out = np.asarray(mat, np.float32).astype(BF16)
    assert np.array_equal(out.astype(np.float64), mat)
    return out


class Level:
    def __init__(self, degree, nx, ny, nz, vecs):
        self.p, self.nx, self.ny, self.nz, self.vecs = degree, nx, ny, nz, vecs
        self.ys = up(nx + 1, 8)
        self.run = up(ny, 8)
        self.base = 2 * self.ys + self.run
        self.rows = up(self.base + nx * self.run, 16)
        self.nb = self.base + self.run
        assert self.nb % 16 == 0
        self.lanes = up(vecs * nz, 128)
        tight = up(self.rows, 16)
        if 3 * tight <= 256:
            self.kp, self.kb = tight, 256
        else:
            self.kp = up(self.rows, 128)
            self.kb = 3 * self.kp
        self.packed = self.kb == 256
        self.seg = 256 if self.packed else self.kp
        self.where = {(x, y): self.row(x, y) for x in range(nx + 1) for y in range(ny + 1)}

    def row(self, x, y):
        if y == 0:
            return x
        if y == self.ny:
            return self.ys + x
        if x == self.nx:
            return 2 * self.ys + y
        return self.base + self.run * x + y

    def factors(self):
        out = []
        for axis, n in ((0, self.nx), (1, self.ny)):
            expand = np.zeros((self.rows, 32))
            spread = np.zeros((128, self.seg))
            for at, row in self.where.items():
                expand[row, at[axis]] = 1
                for copy in range(3 if self.packed else 1):
                    for part in range(3):
                        spread[32 * part + at[axis], copy * self.kp + row] = 1
            table = np.zeros((2, 32, 512), BF16)
            for ghost in range(2):
                for i, element in enumerate(element_matrices(self.p)):
                    parts = bf16_parts(assembled(element, n, ghost), 3)
                    for part, mat in enumerate(parts):
                        at = 128 * i + 32 * part
                        table[ghost, : n + 1, at : at + n + 1] = mat
            out.append((exact_bf16(expand), table, exact_bf16(spread)))
        return out

    def lines(self):
        p, n = self.p, self.nz
        mats = []
        for e in element_matrices(p):
            full = assembled(e, n, True)[:n, :n].T
            if n % 128:
                lifted = np.zeros((self.lanes, self.lanes))
                size = self.vecs * n
                lifted[:size, :size] = np.kron(np.eye(self.vecs), full)
                full = lifted
            mats.append(np.stack(bf16_parts(full, 2)))
        return np.stack(mats)

    def diagonal(self):
        def center(which, count):
            p = self.p
            e = element_matrices(p)[which]
            line = np.array([e[a, a] + (e[p, p] if a == 0 else 0.0) for a in range(p)])
            return line[np.arange(count) % p]

        rows = np.zeros((self.rows, 128), np.float32)
        m_x, m_y, m_z = [center(0, n) for n in (self.nx + self.p, self.ny + self.p, self.nz)]
        k_x, k_y, k_z = [center(1, n) for n in (self.nx + self.p, self.ny + self.p, self.nz)]
        for c in range(3):
            coef = [MU_SHEAR + (LAMBDA_BULK + MU_SHEAR) * (c == e) for e in range(3)]
            for (x, y), row in self.where.items():
                rows[row, c] = coef[0] * k_x[x] * m_y[y] + coef[1] * m_x[x] * k_y[y]
                rows[row, 3 + c] = coef[2] * m_x[x] * m_y[y]
        lanes = np.zeros((8, self.lanes), np.float32)
        lanes[0, : self.vecs * self.nz] = np.tile(m_z, self.vecs)
        lanes[1, : self.vecs * self.nz] = np.tile(k_z, self.vecs)
        return rows, lanes

    def sample(self, top):
        step = top.p // self.p
        sel_x = np.zeros((self.rows, top.rows))
        for (x, y), row in self.where.items():
            sel_x[row, top.where[x * step, y * step]] = 1
        sel_z = np.zeros((top.lanes, self.lanes))
        for v in range(self.vecs):
            for z in range(self.nz):
                sel_z[v * top.nz + z * step, v * self.nz + z] = 1
        return exact_bf16(sel_x), exact_bf16(sel_z)


def interpolation(table, count):
    q = table.shape[0]
    half = q // 2
    out = np.zeros((count + 1, count // 2 + 1))
    for i in range(count + 1):
        for t in range(half + 1):
            j = half * (i // q) + t
            if table[i % q, t] != 0.0:
                out[i, j] += table[i % q, t]
    return out


def transfer(fine, coarse):
    table = PROLONG_TABLES[fine.p]
    px, py = interpolation(table, fine.nx), interpolation(table, fine.ny)
    pz = interpolation(table, fine.nz)[: fine.nz, : coarse.nz]
    plane = np.zeros((fine.rows, coarse.rows))
    for (x, y), row in fine.where.items():
        for (cx, cy), col in coarse.where.items():
            plane[row, col] = px[x, cx] * py[y, cy]
    line = np.zeros((coarse.lanes, fine.lanes))
    size = (fine.vecs * coarse.nz, fine.vecs * fine.nz)
    line[: size[0], : size[1]] = np.kron(np.eye(fine.vecs), pz.T)
    down = (np.tile(plane.T, (1, 2)), np.tile(line.T, (2, 1)))
    upward = (np.tile(plane, (1, 2)), np.tile(line, (2, 1)))
    return [exact_bf16(m) for m in down + upward]


def halves(value):
    hi = value.astype(BF16)
    return hi, (value - hi.astype(F32)).astype(BF16)


def mm(a, b):
    return lax.dot_general(a, b, (((1,), (0,)), ((), ())), preferred_element_type=F32)


def wide3(value):
    hi, lo = halves(value)
    return jnp.concatenate([hi, lo, hi], axis=1)


def wide2(value):
    hi, lo = halves(value)
    return jnp.concatenate([hi, lo], axis=1)


def tall2(value):
    hi, lo = halves(value)
    return jnp.concatenate([hi, lo], axis=0)


def kernel(levels, names, *refs):
    R = dict(zip(names, refs))
    gx_n, gy_n = lax.axis_size("gx"), lax.axis_size("gy")
    me_x, me_y = lax.axis_index("gx"), lax.axis_index("gy")

    def reach(dx, dy):
        ok = None
        for d, me, n in ((dx, me_x, gx_n), (dy, me_y, gy_n)):
            if d:
                here = me + d < n if d > 0 else me + d >= 0
                ok = here if ok is None else jnp.logical_and(ok, here)
        return ok

    def device(dx, dy):
        return (jnp.clip(me_x + dx, 0, gx_n - 1), jnp.clip(me_y + dy, 0, gy_n - 1))

    top = levels[0]
    vecs, nz = top.vecs, top.nz
    body_rows = pl.ds(top.base, top.nx * top.run)

    moves = []

    def load(src, dst):
        moves.append(pltpu.make_async_copy(src, dst, R["lsem"].at[len(moves)]))
        moves[-1].start()

    load(R["moduli_in"], R["moduli"])
    load(R["pinned_in"], R["pinned"])
    for v in range(vecs):
        load(R["modes"].at[v], R["r0"].at[:, body_rows, pl.ds(v * nz, nz)])
    first_moves = len(moves)
    for l, lev in enumerate(levels):
        if lev.nz % 128 == 0:
            R[f"z{l}"][...] = jnp.zeros_like(R[f"z{l}"])
        load(R[f"tx{l}_in"].at[jnp.where(me_x == 0, 1, 0)], R[f"tx{l}"])
        load(R[f"ty{l}_in"].at[jnp.where(me_y == 0, 1, 0)], R[f"ty{l}"])
    for name in names:
        if name.endswith("_in") and name[:2] not in ("mo", "pi", "tx", "ty"):
            if name[0] == "z":
                lev = levels[int(name[1])]
                src, dst = R[name], R[name[:-3]]
                size = lev.nz if lev.nz % 128 == 0 else lev.lanes
                for s, half in enumerate((0, 0, 1)):
                    for at in range(0, lev.lanes, size):
                        load(
                            src.at[:, half],
                            dst.at[:, pl.ds(s * lev.lanes + at, size), pl.ds(at, size)],
                        )
            else:
                load(R[name], R[name[:-3]])

    chebyshev_table(R["spectrum"], R["coef"])
    for l, lev in enumerate(levels):
        for n in "xyd":
            R[f"recv{n}{l}"][...] = jnp.zeros_like(R[f"recv{n}{l}"])
            R[f"send{n}{l}"][...] = jnp.zeros_like(R[f"send{n}{l}"])
        R[f"u{l}"][...] = jnp.zeros_like(R[f"u{l}"])
        R[f"pend{l}"][...] = jnp.zeros_like(R[f"pend{l}"])
    for n in "xyd":
        R[f"got{n}"][...] = jnp.zeros_like(R[f"got{n}"])
    for c in range(3):
        R["r0"][c, 0 : top.base] = jnp.zeros((top.base, top.lanes), F32)

    barrier = pltpu.get_barrier_semaphore()
    for dx, dy in DIRS:

        @pl.when(reach(dx, dy))
        def _():
            pl.semaphore_signal(
                barrier, inc=1, device_id=device(dx, dy), device_id_type=pl.DeviceIdType.MESH
            )

    for one in moves[:first_moves]:
        one.wait()
    scale = R["moduli"][...] * (1.0 - R["pinned"][...].astype(F32))
    s0 = R["s0"]
    s0[0 : top.base] = jnp.zeros((top.base, top.lanes), F32)
    for v in range(vecs):
        s0[body_rows, v * nz : (v + 1) * nz] = scale
    put = R["put"]
    put[...] = jnp.zeros_like(put)
    for c in range(3):
        for x in range(top.nx):
            at = top.base + x * top.run
            put[c, x : x + 1, :] = R["r0"][c, at : at + 1, :]
    for x in range(top.nx):
        at = top.base + x * top.run
        put[3, x : x + 1, :] = s0[at : at + 1, :]
    for c in range(4):
        R["putd"][c : c + 1, :] = put[c, 0:1, :]
    R["putd"][4:8, :] = jnp.zeros((4, top.lanes), F32)
    edge = pl.ds(top.base, top.run)

    def first_copies():
        plan = (
            (-1, 0, R["r0"].at[:, edge, :], R["gotx"].at[pl.ds(0, 3)]),
            (-1, 0, s0.at[edge, :], R["gotx"].at[3]),
            (0, -1, put, R["goty"]),
            (-1, -1, R["putd"], R["gotd"]),
        )
        for i, (dx, dy, src, dst) in enumerate(plan):
            yield dx, dy, pltpu.make_async_remote_copy(
                src_ref=src,
                dst_ref=dst,
                send_sem=R["fsend"].at[i],
                recv_sem=R["frecv"].at[i],
                device_id=device(dx, dy),
                device_id_type=pl.DeviceIdType.MESH,
            )

    around = [
        1 + (me > 0).astype(jnp.int32) + (me < n - 1).astype(jnp.int32)
        for me, n in ((me_x, gx_n), (me_y, gy_n))
    ]
    pl.semaphore_wait(barrier, around[0] * around[1] - 1)
    for dx, dy, copy in first_copies():
        pl.when(reach(dx, dy))(copy.start)
    for one in moves[first_moves:]:
        one.wait()

    def copies(l, slot):
        for i, (dx, dy) in enumerate(DIRS):
            kind, at = ("d", i - 4) if dx and dy else ("x", i) if dx else ("y", i - 2)
            yield dx, dy, pltpu.make_async_remote_copy(
                src_ref=R[f"send{kind}{l}"].at[at],
                dst_ref=R[f"recv{kind}{l}"].at[slot, at],
                send_sem=R[f"ssem{l}"].at[i],
                recv_sem=R[f"rsem{l}"].at[slot, i],
                device_id=device(dx, dy),
                device_id_type=pl.DeviceIdType.MESH,
            )

    def send(l, slot, part):
        lev = levels[l]
        ys, run, nx = lev.ys, lev.run, lev.nx
        sx, sy, sd = (R[f"send{n}{l}"] for n in "xyd")
        tile = 3 * run
        for c in range(3):
            sx[0, c * run : (c + 1) * run] = part[c][lev.base : lev.base + run]
            sx[1, c * run : (c + 1) * run] = part[c][2 * ys : 2 * ys + run]
            low, high = part[c][0:ys], part[c][ys : 2 * ys]
            sx[0, tile + c : tile + c + 1] = low[0:1]
            sx[0, tile + 3 + c : tile + 4 + c] = high[0:1]
            sx[1, tile + c : tile + c + 1] = low[nx : nx + 1]
            sx[1, tile + 3 + c : tile + 4 + c] = high[nx : nx + 1]
            sy[0, c * ys : (c + 1) * ys] = low
            sy[1, c * ys : (c + 1) * ys] = high
            sd[0, 3 + c : 4 + c] = low[0:1]
            sd[1, c : c + 1] = high[0:1]
            sd[2, 3 + c : 4 + c] = low[nx : nx + 1]
            sd[3, c : c + 1] = high[nx : nx + 1]
        for dx, dy, copy in copies(l, slot):
            pl.when(reach(dx, dy))(copy.start)

    def arrive(l, slot):
        lev = levels[l]
        ys, run, nx = lev.ys, lev.run, lev.nx
        for dx, dy, copy in copies(l, slot):
            pl.when(reach(-dx, -dy))(copy.wait_recv)
            pl.when(reach(dx, dy))(copy.wait_send)
        rx, ry, rd = (R[f"recv{n}{l}"] for n in "xyd")
        tile = pl.ds(3 * run, 8)
        left = rx[slot, 1, tile, :] + rd[slot, 2] + rd[slot, 3]
        right = rx[slot, 0, tile, :] + rd[slot, 0] + rd[slot, 1]
        at = lax.broadcasted_iota(jnp.int32, (ys, lev.lanes), 0)
        out = []
        for c in range(3):
            pieces = []
            for k, src in ((0, 1), (1, 0)):
                val = ry[slot, src, c * ys : (c + 1) * ys, :]
                val = val + jnp.where(at == 0, left[3 * k + c : 3 * k + c + 1], 0.0)
                val = val + jnp.where(at == nx, right[3 * k + c : 3 * k + c + 1], 0.0)
                pieces.append(val)
            pieces.append(rx[slot, 0, c * run : (c + 1) * run, :])
            pieces.append(rx[slot, 1, c * run : (c + 1) * run, :])
            out.append(jnp.concatenate(pieces, axis=0))
        return out

    def set_u(l, c, a, b, value):
        lev = levels[l]
        hi, lo = halves(value)
        at = c * lev.kb + a
        R[f"u{l}"][at : at + b - a] = hi
        R[f"u{l}"][at + lev.kp : at + lev.kp + b - a] = hi
        R[f"u{l}"][at + 2 * lev.kp : at + 2 * lev.kp + b - a] = lo

    def span(l, blk):
        lev = levels[l]
        return (0, lev.nb) if blk == "b" else (lev.nb, lev.rows)

    def prepare(l, a, b):
        s = R[f"s{l}"][a:b]
        f = jnp.where(s == 0.0, 1.0, 0.0)
        R[f"f{l}"][a:b] = f
        square = s * s
        m_z, k_z = R[f"kl{l}"][0:1, :], R[f"kl{l}"][1:2, :]
        for c in range(3):
            kd = R[f"kr{l}"][a:b, c : c + 1] * m_z + R[f"kr{l}"][a:b, 3 + c : 4 + c] * k_z
            R[f"dinv{l}"][c, a:b] = 1.0 / (square * kd + f)

    def begin(l, a, b, source):
        scale = R["coef"][l, 12]
        s = R[f"s{l}"][a:b]
        for c in range(3):
            first = scale * (R[f"dinv{l}"][c, a:b] * source[c])
            R[f"r{l}"][c, a:b] = source[c]
            R[f"d{l}"][c, a:b] = first
            R[f"x{l}"][c, a:b] = first
            set_u(l, c, a, b, s * first)

    def local_sums(l, blk):
        lev = levels[l]
        a, b = span(l, blk)
        n, kb = b - a, lev.kb
        u, w1, w2 = R[f"u{l}"], R[f"w1{blk}{l}"], R[f"w2{blk}{l}"]
        both = mm(w1[...], u[0 : 2 * kb])
        last = mm(w2[...], u[2 * kb : 3 * kb])
        mass = w2[3 * n : 4 * n]
        plain = [mm(mass, u[0:kb]), mm(mass, u[kb : 2 * kb]), last[3 * n : 4 * n]]
        stretch = (2.0 * MU_SHEAR + LAMBDA_BULK) / MU_SHEAR
        plain[2] = stretch * plain[2]

        def along(which, parts):
            return mm(jnp.concatenate([wide3(v) for v in parts], axis=0), R[f"z{l}"][which])

        zm = along(M_, [both[0:n], both[n : 2 * n], last[2 * n : 3 * n]])
        zk = along(K_, plain)
        zt = along(T_, [last[0:n], last[n : 2 * n]])
        zg = along(G_, [both[2 * n : 3 * n]])
        return [
            zm[0:n] + zk[0:n] + zt[0:n],
            zm[n : 2 * n] + zk[n : 2 * n] + zt[n : 2 * n],
            zm[2 * n : 3 * n] + zk[2 * n : 3 * n] + zg,
        ]

    def advance(l, k, a, b, sums):
        c1, c2 = R["coef"][l, 2 * k], R["coef"][l, 2 * k + 1]
        s, f = R[f"s{l}"][a:b], R[f"f{l}"][a:b]
        for c in range(3):
            d = R[f"d{l}"][c, a:b]
            res = R[f"r{l}"][c, a:b] - (s * sums[c] + f * d)
            new = c1 * d + c2 * (R[f"dinv{l}"][c, a:b] * res)
            R[f"r{l}"][c, a:b] = res
            R[f"d{l}"][c, a:b] = new
            R[f"x{l}"][c, a:b] += new
            set_u(l, c, a, b, s * new)

    def smooth(l, k, slot, beside=None):
        lev = levels[l]
        own, pend = R[f"own{l}"], R[f"pend{l}"]
        part = local_sums(l, "b")
        for c in range(3):
            part[c] = part[c] + pend[c]
            own[c] = part[c]
            pend[c] = jnp.zeros_like(pend[c])
        send(l, slot, part)
        inner = local_sums(l, "i")
        advance(l, k, lev.nb, lev.rows, inner)
        if beside is not None:
            beside()
        got = arrive(l, slot)
        advance(l, k, 0, lev.nb, [own[c] + got[c] for c in range(3)])

    def restrict(l):
        lev = levels[l]
        masked = []
        for blk in "bi":
            a, b = span(l, blk)
            sums = local_sums(l, blk)
            s, f = R[f"s{l}"][a:b], R[f"f{l}"][a:b]
            free = 1.0 - f
            if blk == "b":
                row = lax.broadcasted_iota(jnp.int32, (b - a, lev.lanes), 0)
                mine = jnp.logical_or(row < lev.nx, row >= lev.base)
                free = jnp.where(mine, free, 0.0)
            piece = []
            for c in range(3):
                r, d = R[f"r{l}"][c, a:b], R[f"d{l}"][c, a:b]
                piece.append(free * r - s * sums[c])
                if blk == "b":
                    R[f"pend{l}"][c] = sums[c]
                    R[f"r{l}"][c, a:b] = r - f * d
                else:
                    R[f"r{l}"][c, a:b] = r - (s * sums[c] + f * d)
            masked.append(piece)
        flat = []
        for c in range(3):
            field = jnp.concatenate([masked[0][c], masked[1][c]], axis=0)
            flat.append(wide2(mm(R[f"dp{l}"][...], tall2(field))))
        down = mm(jnp.concatenate(flat, axis=0), R[f"dz{l}"][...])
        n = levels[l + 1].rows
        return [down[c * n : (c + 1) * n] for c in range(3)]

    def descend(l, slot, sums):
        lev = levels[l]
        own = R[f"own{l}"]
        for c in range(3):
            own[c] = sums[c][0 : lev.nb]
        send(l, slot, [sums[c][0 : lev.nb] for c in range(3)])
        free = 1.0 - R[f"f{l}"][lev.nb : lev.rows]
        begin(l, lev.nb, lev.rows, [free * sums[c][lev.nb : lev.rows] for c in range(3)])
        got = arrive(l, slot)
        free = 1.0 - R[f"f{l}"][0 : lev.nb]
        begin(l, 0, lev.nb, [free * (own[c] + got[c]) for c in range(3)])

    def ascend(l):
        lev, n = levels[l], levels[l + 1].rows
        field = jnp.concatenate([wide2(R[f"x{l + 1}"][c]) for c in range(3)], axis=0)
        fine = mm(field, R[f"uz{l}"][...])
        free, s = 1.0 - R[f"f{l}"][...], R[f"s{l}"][...]
        for c in range(3):
            step = free * mm(R[f"up{l}"][...], tall2(fine[c * n : (c + 1) * n]))
            R[f"d{l}"][c] = step
            R[f"x{l}"][c] += step
            set_u(l, c, 0, lev.rows, s * step)

    def build(l):
        lev = levels[l]
        lines = []
        for axis in "xy":
            tall = mm(R[f"e{axis}{l}"][...], R[f"t{axis}{l}"][...])
            lines.append(
                [
                    mm(tall[:, 128 * i : 128 * (i + 1)].astype(BF16), R[f"c{axis}{l}"][...])
                    for i in range(4)
                ]
            )
        X, Y = lines
        cc = LAMBDA_BULK + MU_SHEAR
        big = MU_SHEAR + cc
        kxmy, mxky = X[K_] * Y[M_], X[M_] * Y[K_]
        first = (
            (0, 0, big * kxmy + MU_SHEAR * mxky),
            (0, 1, cc * (X[G_] * Y[T_])),
            (1, 0, cc * (X[T_] * Y[G_])),
            (1, 1, MU_SHEAR * kxmy + big * mxky),
            (2, 0, cc * (X[T_] * Y[M_])),
            (2, 1, cc * (X[M_] * Y[T_])),
        )
        second = (
            cc * (X[G_] * Y[M_]),
            cc * (X[M_] * Y[G_]),
            MU_SHEAR * (kxmy + mxky),
            X[M_] * Y[M_],
        )
        lane = lax.broadcasted_iota(jnp.int32, (lev.rows, lev.seg), 1)
        middle = jnp.logical_and(lane >= lev.kp, lane < 2 * lev.kp)

        def store(kind, group, at, value):
            hi, lo = halves(value)
            for blk in "bi":
                a, b = span(l, blk)
                ref, row = R[f"{kind}{blk}{l}"], group * (b - a)
                row = slice(row, row + b - a)
                if lev.packed:
                    mixed = jnp.where(middle, lo.astype(F32), hi.astype(F32)).astype(BF16)
                    ref[row, at : at + 256] = mixed[a:b]
                else:
                    for s, half in enumerate((hi, lo, hi)):
                        start = at + s * lev.kp
                        ref[row, start : start + lev.kp] = half[a:b]

        for group, side, value in first:
            store("w1", group, side * lev.kb, value)
        for group, value in enumerate(second):
            store("w2", group, 0, value)

    build(0)

    def clear_spare(a, b):
        lead = lax.broadcasted_iota(jnp.int32, (b - a, top.lanes), 0) % top.run == 0
        s0[a:b] = jnp.where(lead, 0.0, s0[a:b])

    clear_spare(top.nb, top.rows)
    prepare(0, top.nb, top.rows)
    begin(0, top.nb, top.rows, [R["r0"][c, top.nb : top.rows] for c in range(3)])
    for dx, dy, copy in first_copies():
        pl.when(reach(dx, dy))(copy.wait_send)
        pl.when(reach(-dx, -dy))(copy.wait_recv)
    clear_spare(top.base, top.nb)
    ys, run, nx = top.ys, top.run, top.nx
    at = lax.broadcasted_iota(jnp.int32, (ys, top.lanes), 0)
    for c in range(4):
        dst = s0 if c == 3 else R["r0"].at[c]
        low = jnp.where(at == nx, R["gotx"][c, 0:1, :], put[c])
        high = jnp.where(at == nx, R["gotd"][c : c + 1, :], R["goty"][c])
        dst[0:ys] = low
        dst[ys : 2 * ys] = high
        side = R["gotx"][c]
        if c == 3:
            row = lax.broadcasted_iota(jnp.int32, (run, top.lanes), 0)
            side = jnp.where(row == 0, 0.0, side)
        dst[2 * ys : 2 * ys + run] = side
    prepare(0, 0, top.nb)
    begin(0, 0, top.nb, [R["r0"][c, 0 : top.nb] for c in range(3)])

    def coarse_setup():
        whole = s0[...]
        parts = []
        rest = whole
        for _ in range(3):
            part = rest.astype(BF16)
            parts.append(part)
            rest = rest - part.astype(F32)
        for l in range(1, len(levels)):
            sel_x, sel_z = R[f"sx{l}"][...], R[f"sz{l}"][...]
            picked = [mm(sel_x, part).astype(BF16) for part in parts]
            R[f"s{l}"][...] = sum(mm(part, sel_z) for part in picked)
            prepare(l, 0, levels[l].rows)
            build(l)

    def pre(k, _):
        smooth(0, k, k % 2, lambda: pl.when(k == 0)(coarse_setup))
        return 0

    def cycle(l):
        last = l == len(levels) - 1
        skip = 0 if l == 0 else 1

        def body(k, _):
            smooth(l, k, (k + skip) % 2)
            return 0

        def tail(k, _):
            smooth(l, k, (k + skip + 1) % 2)
            return 0

        if last:
            lax.fori_loop(0, COARSE_DEG - 1, body, 0)
            return
        lax.fori_loop(0, DEG - 1, pre if l == 0 else body, 0)
        descend(l + 1, 0, restrict(l))
        cycle(l + 1)
        ascend(l)
        lax.fori_loop(DEG, 2 * DEG, tail, 0)

    cycle(0)
    for c in range(3):
        for x in range(nx):
            row = top.base + x * run
            R["x0"][c, row : row + 1, :] = R["x0"][c, x : x + 1, :]
    backs = [
        pltpu.make_async_copy(
            R["x0"].at[:, body_rows, pl.ds(v * nz, nz)], R["out"].at[v], R["lsem"].at[v]
        )
        for v in range(vecs)
    ]
    for one in backs:
        one.start()
    for one in backs:
        one.wait()


def chebyshev_table(spectrum, coef):
    for l in range(3):
        low, top = spectrum[l, 0], spectrum[l, 1]
        center = 0.5 * (top + low)
        radius = 0.5 * (top - low)
        ratio = center / radius
        rho = 1.0 / ratio
        steps = []
        for _ in range(COARSE_DEG - 1):
            rho_next = 1.0 / (2.0 * ratio - rho)
            steps.append((rho_next * rho, 2.0 * rho_next / radius))
            rho = rho_next
        smooth = steps[: DEG - 1]
        flat = [(0.0, 0.0), (0.0, 1.0 / center)]
        picked = steps if l == 2 else smooth + flat + smooth
        for k, two in enumerate(picked):
            coef[l, 2 * k] = jnp.asarray(two[0], F32)
            coef[l, 2 * k + 1] = jnp.asarray(two[1], F32)
        coef[l, 12] = 1.0 / center


def local(modes, moduli, pinned, spectrum):
    vecs, _, nx, ny, nz = modes.shape
    levels = []
    names, args = [], []

    def add(name, value):
        names.append(name)
        args.append(value)

    for degree in DEGREES:
        step = DEGREES[0] // degree
        levels.append(Level(degree, nx // step, ny // step, nz // step, vecs))
    top = levels[0]
    assert ny == top.run and nz % 128 == 0
    add("spectrum", spectrum)
    add("modes", modes.reshape(vecs, 3, nx * ny, nz))
    add("moduli_in", moduli.reshape(nx * ny, nz))
    add("pinned_in", pinned.reshape(nx * ny, nz))
    for l, lev in enumerate(levels):
        for axis, mats in zip("xy", lev.factors()):
            for key, mat in zip("etc", mats):
                add(f"{key}{axis}{l}_in", jnp.asarray(mat))
        add(f"z{l}_in", jnp.asarray(lev.lines()))
        for key, mat in zip(("kr", "kl"), lev.diagonal()):
            add(f"{key}{l}_in", jnp.asarray(mat))
        if l + 1 < len(levels):
            for key, mat in zip(("dp", "dz", "up", "uz"), transfer(lev, levels[l + 1])):
                add(f"{key}{l}_in", jnp.asarray(mat))
        if l:
            for key, mat in zip(("sx", "sz"), lev.sample(top)):
                add(f"{key}{l}_in", jnp.asarray(mat))

    specs = [
        pl.BlockSpec(memory_space=pltpu.SMEM if n == "spectrum" else pl.ANY) for n in names
    ]
    scratch = []
    all_names = names + ["out"]

    def temp(name, what):
        all_names.append(name)
        scratch.append(what)

    temp("coef", pltpu.SMEM((3, 13), F32))
    temp("lsem", pltpu.SemaphoreType.DMA((len(names) + 24,)))
    for name, value in zip(names, args):
        if name.endswith("_in"):
            shape = value.shape
            if name[0] == "z":
                lanes = levels[int(name[1])].lanes
                shape = (4, 3 * lanes, lanes)
            elif name[0] == "t":
                shape = shape[1:]
            temp(name[:-3], pltpu.VMEM(shape, value.dtype))
    for l, lev in enumerate(levels):
        field = (3, lev.rows, lev.lanes)
        for n in ("s", "f"):
            temp(f"{n}{l}", pltpu.VMEM(field[1:], F32))
        for n in ("r", "d", "x", "dinv"):
            temp(f"{n}{l}", pltpu.VMEM(field, F32))
        for n in ("own", "pend"):
            temp(f"{n}{l}", pltpu.VMEM((3, lev.nb, lev.lanes), F32))
        temp(f"u{l}", pltpu.VMEM((3 * lev.kb, lev.lanes), BF16))
        for blk, n in (("b", lev.nb), ("i", lev.rows - lev.nb)):
            temp(f"w1{blk}{l}", pltpu.VMEM((3 * n, 2 * lev.kb), BF16))
            temp(f"w2{blk}{l}", pltpu.VMEM((4 * n, lev.kb), BF16))
        for n, shape in (
            ("x", (2, 3 * lev.run + 8, lev.lanes)),
            ("y", (2, 3 * lev.ys, lev.lanes)),
            ("d", (4, 8, lev.lanes)),
        ):
            temp(f"send{n}{l}", pltpu.VMEM(shape, F32))
            temp(f"recv{n}{l}", pltpu.VMEM((2,) + shape, F32))
        temp(f"ssem{l}", pltpu.SemaphoreType.DMA((len(DIRS),)))
        temp(f"rsem{l}", pltpu.SemaphoreType.DMA((2, len(DIRS))))
    temp("put", pltpu.VMEM((4, top.ys, top.lanes), F32))
    temp("putd", pltpu.VMEM((8, top.lanes), F32))
    temp("gotx", pltpu.VMEM((4, top.run, top.lanes), F32))
    temp("goty", pltpu.VMEM((4, top.ys, top.lanes), F32))
    temp("gotd", pltpu.VMEM((8, top.lanes), F32))
    temp("fsend", pltpu.SemaphoreType.DMA((4,)))
    temp("frecv", pltpu.SemaphoreType.DMA((4,)))
    out = pl.pallas_call(
        functools.partial(kernel, levels, all_names),
        out_shape=jax.ShapeDtypeStruct((vecs, 3, nx * ny, nz), F32),
        in_specs=specs,
        out_specs=pl.BlockSpec(memory_space=pl.ANY),
        scratch_shapes=scratch,
        compiler_params=pltpu.CompilerParams(
            collective_id=0, has_side_effects=True, vmem_limit_bytes=60 * 1024 * 1024
        ),
    )(*args)
    return out.reshape(modes.shape)


def solution(mesh):
    placed = (P(None, None, "gx", "gy", None), P("gx", "gy", None), P("gx", "gy", None), P())
    return jax.shard_map(
        local,
        mesh=mesh,
        in_specs=placed,
        out_specs=P(None, None, "gx", "gy", None),
        check_vma=False,
    )
```

time: 148 us -> 86 us (0.58)
  Pallas kernels: 137 us -> 82.5 us
  local copies, waits for them, and re-layouts: 9.98 us -> 3.28 us
    pallas_call x1, Pallas kernels: 137 us -> 82.5 us  [local(): pl.pallas_call(functools.partial(kernel, levels, all_names), out_shape=ja...]
    another operation x11 -> x0, local copies, waits for them, and re-layouts: 6.7 us -> none
    unnamed x2 -> x4, local copies, waits for them, and re-layouts: 3.28 us -> 3.28 us
where the time goes in v1:
time: 86 us; the launch traced here: 85.8 us
  Pallas kernels  82.5 us (96%)
  local copies, waits for them, and re-layouts  3.28 us (4%)
    pallas_call x1, Pallas kernels, local(): pl.pallas_call(functools.partial(kernel, levels, all_names), out_shape=ja...  82.5 us
    unnamed x4, local copies, waits for them, and re-layouts  3.28 us

profile of v1, /device:TPU:17, one launch (start us, length us, event | category | flops | bytes accessed | tf_op | source)
XLA Modules:
  0.0 85.8 jit_solution(8680539743665007953)
XLA Ops:
  0.0 0.0 copy-start
  0.0 0.7 copy-done
  0.7 0.7 copy.44.refs_0_
  1.3 82.5 %shard_map.397 = f32[2,3,192,128]{3,2,1,0:T(8,128)} custom-call(f32[3,2]{1,0:T(4,128)} %copy.44.refs_0_, f32[2,3,192,128]{3,2,1,0:T(8,128)} %bitcast.5, f32[192,128]{1,0:T(8,128)} %bitcast.6, s32[192,128]{1,0:T(8,128)} %bitcast.7, bf16[240,32]{1,0:T(8,128)(2,1)} %constant.78.clone.refs_4_, bf16[2,32,512]{2,1,0:T(8,128)(2,1)} %constant.79.clone.refs_5_, ...), custom_call_target="tpu_custom_call" | custom-call | tf_op jit(solution)/shard_map/pallas_call | solution.py:785
  83.8 1.9 %copy.46 = f32[2,3,12,16,128]{4,3,2,1,0:T(8,128)} copy(f32[2,3,12,16,128]{4,3,2,1,0:T(8,128)} %bitcast.4) | data formatting | bytes 1179648
Async XLA Ops:
  0.0 0.7 copy-start

commit v2 on v1

--- a/solution.py
+++ b/solution.py
@@ -91,15 +91,19 @@
         self.nb = self.base + self.run
         assert self.nb % 16 == 0
         self.lanes = up(vecs * nz, 128)
-        tight = up(self.rows, 16)
-        if 3 * tight <= 256:
-            self.kp, self.kb = tight, 256
+        self.low = 0
+        self.where = {(x, y): self.row(x, y) for x in range(nx + 1) for y in range(ny + 1)}
+        self.spans = (nx, ny)
+        self.columns()
+
+    def columns(self):
+        if 3 * self.rows <= 256:
+            self.kp, self.kb = self.rows, 256
         else:
             self.kp = up(self.rows, 128)
             self.kb = 3 * self.kp
         self.packed = self.kb == 256
         self.seg = 256 if self.packed else self.kp
-        self.where = {(x, y): self.row(x, y) for x in range(nx + 1) for y in range(ny + 1)}
 
     def row(self, x, y):
         if y == 0:
@@ -112,14 +116,14 @@
 
     def factors(self):
         out = []
-        for axis, n in ((0, self.nx), (1, self.ny)):
+        for axis, n in enumerate(self.spans):
             expand = np.zeros((self.rows, 32))
             spread = np.zeros((128, self.seg))
             for at, row in self.where.items():
-                expand[row, at[axis]] = 1
+                expand[row, at[axis] + self.low] = 1
                 for copy in range(3 if self.packed else 1):
                     for part in range(3):
-                        spread[32 * part + at[axis], copy * self.kp + row] = 1
+                        spread[32 * part + at[axis] + self.low, copy * self.kp + row] = 1
             table = np.zeros((2, 32, 512), BF16)
             for ghost in range(2):
                 for i, element in enumerate(element_matrices(self.p)):
@@ -156,6 +160,7 @@
         for c in range(3):
             coef = [MU_SHEAR + (LAMBDA_BULK + MU_SHEAR) * (c == e) for e in range(3)]
             for (x, y), row in self.where.items():
+                x, y = x % self.p, y % self.p
                 rows[row, c] = coef[0] * k_x[x] * m_y[y] + coef[1] * m_x[x] * k_y[y]
                 rows[row, 3 + c] = coef[2] * m_x[x] * m_y[y]
         lanes = np.zeros((8, self.lanes), np.float32)
@@ -167,12 +172,119 @@
         step = top.p // self.p
         sel_x = np.zeros((self.rows, top.rows))
         for (x, y), row in self.where.items():
-            sel_x[row, top.where[x * step, y * step]] = 1
+            if (x * step, y * step) in top.where:
+                sel_x[row, top.where[x * step, y * step]] = 1
         sel_z = np.zeros((top.lanes, self.lanes))
         for v in range(self.vecs):
             for z in range(self.nz):
                 sel_z[v * top.nz + z * step, v * self.nz + z] = 1
         return exact_bf16(sel_x), exact_bf16(sel_z)
+
+
+class Wide(Level):
+    def __init__(self, degree, nx, ny, nz, vecs, ring):
+        self.p, self.nx, self.ny, self.nz, self.vecs = degree, nx, ny, nz, vecs
+        self.low = ring * degree
+        self.spans = (nx + 2 * self.low, ny + 2 * self.low)
+        self.lanes = up(vecs * nz, 128)
+        self.half = self.lanes // 2
+        assert vecs * nz <= self.half
+        self.where = {}
+        for x in range(-self.low, nx + self.low + 1):
+            for y in range(-self.low, ny + self.low + 1):
+                self.where[x, y] = len(self.where)
+        self.rows = up(len(self.where), 16)
+        self.nb = 0
+        self.columns()
+        self.plan()
+
+    def plan(self):
+        nx, ny, low = self.nx, self.ny, self.low
+        closed = [(x, y) for x in range(nx + 1) for y in range(ny + 1)]
+        far = [-(-(low + 1) // n) for n in (nx, ny)]
+        self.far = far
+        self.sections, self.sends = [], []
+        self.pack_rows = 0
+        at = 0
+        kinds = {}
+        for dx in range(-far[0], far[0] + 1):
+            for dy in range(-far[1], far[1] + 1):
+                nodes = tuple(
+                    (x, y) for x, y in closed if (x - dx * nx, y - dy * ny) in self.where
+                )
+                if abs(dx) <= 1 and abs(dy) <= 1:
+                    nodes = tuple(closed)
+                if not nodes:
+                    continue
+                if nodes not in kinds:
+                    k = len(nodes)
+                    size = up(k + -(-k // 2), 8)
+                    kinds[nodes] = (self.pack_rows, size)
+                    self.sections.append((self.pack_rows, size, nodes))
+                    self.pack_rows += size
+                start, size = kinds[nodes]
+                self.sends.append((dx, dy, start, size, at, nodes))
+                at += size
+        self.pack_rows = up(self.pack_rows, 16)
+        self.got_rows = up(at, 16)
+
+    def gather(self, fine, top):
+        table = PROLONG_TABLES[fine.p]
+        px, py = interpolation(table, fine.nx), interpolation(table, fine.ny)
+        plane = {
+            (cx, cy): np.array(
+                [
+                    [px[x, cx] * py[y, cy], row]
+                    for (x, y), row in fine.where.items()
+                    if px[x, cx] * py[y, cy] != 0.0
+                ]
+            )
+            for cx in range(self.nx + 1)
+            for cy in range(self.ny + 1)
+        }
+        pack = np.zeros((2, self.pack_rows, 4 * fine.rows))
+        scale = np.zeros((self.pack_rows, top.rows))
+        step = top.p // self.p
+        for start, size, nodes in self.sections:
+            k = len(nodes)
+            h = -(-k // 2)
+            for i, node in enumerate(nodes):
+                for weight, row in plane[node]:
+                    row = int(row)
+                    for side in range(2):
+                        pack[side, start + i, row] = weight
+                        pack[side, start + i, fine.rows + row] = weight
+                    side = i // h
+                    pack[side, start + k + i % h, 2 * fine.rows + row] = weight
+                    pack[side, start + k + i % h, 3 * fine.rows + row] = weight
+                if node[0] < self.nx and node[1] < self.ny:
+                    scale[start + i, top.where[node[0] * step, node[1] * step]] = 1
+        place = np.zeros((3, self.rows, self.got_rows))
+        for dx, dy, start, size, at, nodes in self.sends:
+            k = len(nodes)
+            h = -(-k // 2)
+            for i, (x, y) in enumerate(nodes):
+                to = self.where.get((x - dx * self.nx, y - dy * self.ny))
+                if to is not None:
+                    place[0, to, at + i] = 1
+                    place[1 + i // h, to, at + k + i % h] = 1
+        down = interpolation(table, fine.nz)[: fine.nz, : self.nz]
+        line = np.zeros((2, 2 * fine.lanes, self.lanes))
+        size = (self.vecs * fine.nz, self.vecs * self.nz)
+        for side in range(2):
+            for copy in range(2):
+                line[
+                    side,
+                    copy * fine.lanes : copy * fine.lanes + size[0],
+                    side * self.half : side * self.half + size[1],
+                ] = np.kron(np.eye(self.vecs), down)
+        mats = (
+            pack.reshape(2 * self.pack_rows, 4 * fine.rows),
+            scale,
+            place.reshape(3 * self.rows, self.got_rows),
+            line.reshape(4 * fine.lanes, self.lanes),
+        )
+        return [exact_bf16(m) for m in mats]
 
 
 def interpolation(table, count):
@@ -194,7 +306,8 @@
     plane = np.zeros((fine.rows, coarse.rows))
     for (x, y), row in fine.where.items():
         for (cx, cy), col in coarse.where.items():
-            plane[row, col] = px[x, cx] * py[y, cy]
+            if 0 <= cx <= coarse.nx and 0 <= cy <= coarse.ny:
+                plane[row, col] = px[x, cx] * py[y, cy]
     line = np.zeros((coarse.lanes, fine.lanes))
     size = (fine.vecs * coarse.nz, fine.vecs * fine.nz)
     line[: size[0], : size[1]] = np.kron(np.eye(fine.vecs), pz.T)
@@ -255,6 +368,7 @@
 
     load(R["moduli_in"], R["moduli"])
     load(R["pinned_in"], R["pinned"])
+    load(R["spectrum_in"], R["spectrum"])
     for v in range(vecs):
         load(R["modes"].at[v], R["r0"].at[:, body_rows, pl.ds(v * nz, nz)])
     first_moves = len(moves)
@@ -264,7 +378,7 @@
         load(R[f"tx{l}_in"].at[jnp.where(me_x == 0, 1, 0)], R[f"tx{l}"])
         load(R[f"ty{l}_in"].at[jnp.where(me_y == 0, 1, 0)], R[f"ty{l}"])
     for name in names:
-        if name.endswith("_in") and name[:2] not in ("mo", "pi", "tx", "ty"):
+        if name.endswith("_in") and name[:2] not in ("mo", "pi", "sp", "tx", "ty"):
             if name[0] == "z":
                 lev = levels[int(name[1])]
                 src, dst = R[name], R[name[:-3]]
@@ -278,20 +392,22 @@
             else:
                 load(R[name], R[name[:-3]])
 
-    chebyshev_table(R["spectrum"], R["coef"])
-    for l, lev in enumerate(levels):
+    wide = levels[-1]
+    edged = range(len(levels) - 1)
+
+    def clear(name):
+        R[name][...] = jnp.zeros_like(R[name])
+
+    for l in edged:
         for n in "xyd":
-            R[f"recv{n}{l}"][...] = jnp.zeros_like(R[f"recv{n}{l}"])
-            R[f"send{n}{l}"][...] = jnp.zeros_like(R[f"send{n}{l}"])
-        R[f"u{l}"][...] = jnp.zeros_like(R[f"u{l}"])
-        R[f"pend{l}"][...] = jnp.zeros_like(R[f"pend{l}"])
-    for n in "xyd":
-        R[f"got{n}"][...] = jnp.zeros_like(R[f"got{n}"])
-    for c in range(3):
-        R["r0"][c, 0 : top.base] = jnp.zeros((top.base, top.lanes), F32)
+            clear(f"recv{n}{l}")
+    for n in ("gotx", "goty", "gotd", "gets", "getb"):
+        clear(n)
 
     barrier = pltpu.get_barrier_semaphore()
-    for dx, dy in DIRS:
+    peers = [(dx, dy) for dx, dy, *_ in wide.sends if dx or dy]
+    assert set(DIRS) <= set(peers)
+    for dx, dy in peers:
 
         @pl.when(reach(dx, dy))
         def _():
@@ -299,8 +415,16 @@
                 barrier, inc=1, device_id=device(dx, dy), device_id_type=pl.DeviceIdType.MESH
             )
 
+    for l in edged:
+        for n in "xyd":
+            clear(f"send{n}{l}")
+        clear(f"pend{l}")
+    for l in range(len(levels)):
+        clear(f"u{l}")
+
     for one in moves[:first_moves]:
         one.wait()
+    chebyshev_table(R["spectrum"], R["coef"])
     scale = R["moduli"][...] * (1.0 - R["pinned"][...].astype(F32))
     s0 = R["s0"]
     s0[0 : top.base] = jnp.zeros((top.base, top.lanes), F32)
@@ -337,10 +461,9 @@
                 device_id_type=pl.DeviceIdType.MESH,
             )
 
-    around = [
-        1 + (me > 0).astype(jnp.int32) + (me < n - 1).astype(jnp.int32)
-        for me, n in ((me_x, gx_n), (me_y, gy_n))
-    ]
+    around = []
+    for me, n, far in ((me_x, gx_n, wide.far[0]), (me_y, gy_n, wide.far[1])):
+        around.append(1 + jnp.minimum(me, far) + jnp.minimum(n - 1 - me, far))
     pl.semaphore_wait(barrier, around[0] * around[1] - 1)
     for dx, dy, copy in first_copies():
         pl.when(reach(dx, dy))(copy.start)
@@ -405,6 +528,53 @@
             out.append(jnp.concatenate(pieces, axis=0))
         return out
 
+    def wide_copies(kind):
+        index = 0
+        for dx, dy, start, size, at, nodes in wide.sends:
+            if dx == 0 and dy == 0:
+                continue
+            count = up(len(nodes), 8) if kind == "s" else size
+            yield dx, dy, pltpu.make_async_remote_copy(
+                src_ref=R[f"pack{kind}"].at[pl.ds(start, count)],
+                dst_ref=R[f"get{kind}"].at[pl.ds(at, count)],
+                send_sem=R[f"wsend{kind}"].at[index],
+                recv_sem=R[f"wrecv{kind}"].at[index],
+                device_id=device(dx, dy),
+                device_id_type=pl.DeviceIdType.MESH,
+            )
+            index += 1
+
+    def wide_send(kind, value):
+        R[f"pack{kind}"][...] = value
+        for dx, dy, start, size, at, nodes in wide.sends:
+            if dx == 0 and dy == 0:
+                R[f"get{kind}"][at : at + size] = value[start : start + size]
+        for dx, dy, copy in wide_copies(kind):
+            pl.when(reach(dx, dy))(copy.start)
+
+    def wide_wait(kind):
+        for dx, dy, copy in wide_copies(kind):
+            pl.when(reach(-dx, -dy))(copy.wait_recv)
+            pl.when(reach(dx, dy))(copy.wait_send)
+
+    def thirds(value):
+        parts = []
+        for _ in range(3):
+            parts.append(value.astype(BF16))
+            value = value - parts[-1].astype(F32)
+        return parts
+
+    def wide_scale_send():
+        sel = R["gs"][...]
+        picked = [mm(sel, part).astype(BF16) for part in thirds(s0[...])]
+        wide_send("s", sum(mm(part, R["sz"][...]) for part in picked))
+
+    def wide_scale_take():
+        wide_wait("s")
+        place = R["place"][0 : wide.rows]
+        R[f"s{len(levels) - 1}"][...] = sum(mm(place, part) for part in thirds(R["gets"][...]))
+        prepare(len(levels) - 1, 0, wide.rows)
+
     def set_u(l, c, a, b, value):
         lev = levels[l]
         hi, lo = halves(value)
@@ -512,10 +682,18 @@
                 else:
                     R[f"r{l}"][c, a:b] = r - (s * sums[c] + f * d)
             masked.append(piece)
-        flat = []
-        for c in range(3):
-            field = jnp.concatenate([masked[0][c], masked[1][c]], axis=0)
-            flat.append(wide2(mm(R[f"dp{l}"][...], tall2(field))))
+        fields = [
+            tall2(jnp.concatenate([masked[0][c], masked[1][c]], axis=0)) for c in range(3)
+        ]
+        if l + 1 == len(levels) - 1:
+            n = wide.pack_rows
+            flat = []
+            for side in range(2):
+                mat = R["gp"][side * n : (side + 1) * n]
+                field = jnp.concatenate([fields[side], fields[2]], axis=0)
+                flat.append(wide2(mm(mat, field)))
+            return mm(jnp.concatenate(flat, axis=1), R["gz"][...])
+        flat = [wide2(mm(R[f"dp{l}"][...], field)) for field in fields]
         down = mm(jnp.concatenate(flat, axis=0), R[f"dz{l}"][...])
         n = levels[l + 1].rows
         return [down[c * n : (c + 1) * n] for c in range(3)]
@@ -528,9 +706,29 @@
         send(l, slot, [sums[c][0 : lev.nb] for c in range(3)])
         free = 1.0 - R[f"f{l}"][lev.nb : lev.rows]
         begin(l, lev.nb, lev.rows, [free * sums[c][lev.nb : lev.rows] for c in range(3)])
+        if l + 1 == len(levels) - 1:
+            wide_scale_take()
         got = arrive(l, slot)
         free = 1.0 - R[f"f{l}"][0 : lev.nb]
         begin(l, 0, lev.nb, [free * (own[c] + got[c]) for c in range(3)])
+
+    def solve_wide(packed):
+        l, n, half = len(levels) - 1, wide.rows, wide.half
+        wide_send("b", packed)
+        wide_wait("b")
+        hi, lo = halves(R["getb"][...])
+        spread = mm(R["place"][...], hi) + mm(R["place"][...], lo)
+        lane = lax.broadcasted_iota(jnp.int32, (n, wide.lanes), 1)
+        keep = jnp.where(lane < half, 1.0 - R[f"f{l}"][...], 0.0)
+        both, one, two = (spread[i * n : (i + 1) * n] for i in range(3))
+        right = [both, pltpu.roll(both, half, 1), one + pltpu.roll(two, half, 1)]
+        begin(l, 0, n, [keep * v for v in right])
+
+        def body(k, _):
+            advance(l, k, 0, n, local_sums(l, "i"))
+            return 0
+
+        lax.fori_loop(0, COARSE_DEG - 1, body, 0)
 
     def ascend(l):
         lev, n = levels[l], levels[l + 1].rows
@@ -577,7 +775,7 @@
 
         def store(kind, group, at, value):
             hi, lo = halves(value)
-            for blk in "bi":
+            for blk in "bi" if lev.nb else "i":
                 a, b = span(l, blk)
                 ref, row = R[f"{kind}{blk}{l}"], group * (b - a)
                 row = slice(row, row + b - a)
@@ -624,14 +822,9 @@
     begin(0, 0, top.nb, [R["r0"][c, 0 : top.nb] for c in range(3)])
 
     def coarse_setup():
-        whole = s0[...]
-        parts = []
-        rest = whole
-        for _ in range(3):
-            part = rest.astype(BF16)
-            parts.append(part)
-            rest = rest - part.astype(F32)
-        for l in range(1, len(levels)):
+        parts = thirds(s0[...])
+        build(len(levels) - 1)
+        for l in range(1, len(levels) - 1):
             sel_x, sel_z = R[f"sx{l}"][...], R[f"sz{l}"][...]
             picked = [mm(sel_x, part).astype(BF16) for part in parts]
             R[f"s{l}"][...] = sum(mm(part, sel_z) for part in picked)
@@ -643,7 +836,6 @@
         return 0
 
     def cycle(l):
-        last = l == len(levels) - 1
         skip = 0 if l == 0 else 1
 
         def body(k, _):
@@ -654,12 +846,14 @@
             smooth(l, k, (k + skip + 1) % 2)
             return 0
 
-        if last:
-            lax.fori_loop(0, COARSE_DEG - 1, body, 0)
-            return
         lax.fori_loop(0, DEG - 1, pre if l == 0 else body, 0)
-        descend(l + 1, 0, restrict(l))
-        cycle(l + 1)
+        if l == 0:
+            wide_scale_send()
+        if l + 1 == len(levels) - 1:
+            solve_wide(restrict(l))
+        else:
+            descend(l + 1, 0, restrict(l))
+            cycle(l + 1)
         ascend(l)
         lax.fori_loop(DEG, 2 * DEG, tail, 0)
 
@@ -712,10 +906,11 @@
 
     for degree in DEGREES:
         step = DEGREES[0] // degree
-        levels.append(Level(degree, nx // step, ny // step, nz // step, vecs))
+        size = (degree, nx // step, ny // step, nz // step, vecs)
+        levels.append(Level(*size) if step < DEGREES[0] else Wide(*size, COARSE_DEG - 1))
     top = levels[0]
     assert ny == top.run and nz % 128 == 0
-    add("spectrum", spectrum)
+    add("spectrum_in", spectrum)
     add("modes", modes.reshape(vecs, 3, nx * ny, nz))
     add("moduli_in", moduli.reshape(nx * ny, nz))
     add("pinned_in", pinned.reshape(nx * ny, nz))
@@ -727,15 +922,19 @@
         for key, mat in zip(("kr", "kl"), lev.diagonal()):
             add(f"{key}{l}_in", jnp.asarray(mat))
         if l + 1 < len(levels):
+            coarsest = l + 2 == len(levels)
             for key, mat in zip(("dp", "dz", "up", "uz"), transfer(lev, levels[l + 1])):
-                add(f"{key}{l}_in", jnp.asarray(mat))
-        if l:
+                if key[0] == "u" or not coarsest:
+                    add(f"{key}{l}_in", jnp.asarray(mat))
+        if 0 < l < len(levels) - 1:
             for key, mat in zip(("sx", "sz"), lev.sample(top)):
                 add(f"{key}{l}_in", jnp.asarray(mat))
-
-    specs = [
-        pl.BlockSpec(memory_space=pltpu.SMEM if n == "spectrum" else pl.ANY) for n in names
-    ]
+    wide = levels[-1]
+    for key, mat in zip(("gp", "gs", "place", "gz"), wide.gather(levels[-2], top)):
+        add(f"{key}_in", jnp.asarray(mat))
+    add("sz_in", jnp.asarray(wide.sample(top)[1]))
+
+    specs = [pl.BlockSpec(memory_space=pl.ANY) for n in names]
     scratch = []
     all_names = names + ["out"]
 
@@ -746,7 +945,9 @@
     temp("coef", pltpu.SMEM((3, 13), F32))
     temp("lsem", pltpu.SemaphoreType.DMA((len(names) + 24,)))
     for name, value in zip(names, args):
-        if name.endswith("_in"):
+        if name == "spectrum_in":
+            temp("spectrum", pltpu.SMEM(value.shape, F32))
+        elif name.endswith("_in"):
             shape = value.shape
             if name[0] == "z":
                 lanes = levels[int(name[1])].lanes
@@ -760,12 +961,15 @@
             temp(f"{n}{l}", pltpu.VMEM(field[1:], F32))
         for n in ("r", "d", "x", "dinv"):
             temp(f"{n}{l}", pltpu.VMEM(field, F32))
+        temp(f"u{l}", pltpu.VMEM((3 * lev.kb, lev.lanes), BF16))
+        for blk, n in (("b", lev.nb), ("i", lev.rows - lev.nb)):
+            if n:
+                temp(f"w1{blk}{l}", pltpu.VMEM((3 * n, 2 * lev.kb), BF16))
+                temp(f"w2{blk}{l}", pltpu.VMEM((4 * n, lev.kb), BF16))
+        if lev is wide:
+            continue
         for n in ("own", "pend"):
             temp(f"{n}{l}", pltpu.VMEM((3, lev.nb, lev.lanes), F32))
-        temp(f"u{l}", pltpu.VMEM((3 * lev.kb, lev.lanes), BF16))
-        for blk, n in (("b", lev.nb), ("i", lev.rows - lev.nb)):
-            temp(f"w1{blk}{l}", pltpu.VMEM((3 * n, 2 * lev.kb), BF16))
-            temp(f"w2{blk}{l}", pltpu.VMEM((4 * n, lev.kb), BF16))
         for n, shape in (
             ("x", (2, 3 * lev.run + 8, lev.lanes)),
             ("y", (2, 3 * lev.ys, lev.lanes)),
@@ -775,6 +979,11 @@
             temp(f"recv{n}{l}", pltpu.VMEM((2,) + shape, F32))
         temp(f"ssem{l}", pltpu.SemaphoreType.DMA((len(DIRS),)))
         temp(f"rsem{l}", pltpu.SemaphoreType.DMA((2, len(DIRS))))
+    for kind in "sb":
+        temp(f"pack{kind}", pltpu.VMEM((wide.pack_rows, wide.lanes), F32))
+        temp(f"get{kind}", pltpu.VMEM((wide.got_rows, wide.lanes), F32))
+        temp(f"wsend{kind}", pltpu.SemaphoreType.DMA((len(wide.sends) - 1,)))
+        temp(f"wrecv{kind}", pltpu.SemaphoreType.DMA((len(wide.sends) - 1,)))
     temp("put", pltpu.VMEM((4, top.ys, top.lanes), F32))
     temp("putd", pltpu.VMEM((8, top.lanes), F32))
     temp("gotx", pltpu.VMEM((4, top.run, top.lanes), F32))

time: 86 us -> 77.8 us (0.905)
  Pallas kernels: 82.5 us -> 73.7 us
    pallas_call x1, Pallas kernels: 82.5 us -> 73.7 us  [local(): pl.pallas_call(functools.partial(kernel, levels, all_names), out_shape=ja...]
where the time goes in v2:
time: 77.8 us; the launch traced here: 77 us
  Pallas kernels  73.7 us (95%)
  local copies, waits for them, and re-layouts  3.28 us (4%)
    pallas_call x1, Pallas kernels, local(): pl.pallas_call(functools.partial(kernel, levels, all_names), out_shape=ja...  73.7 us
    unnamed x4, local copies, waits for them, and re-layouts  3.28 us

profile of v2, /device:TPU:17, one launch (start us, length us, event | category | flops | bytes accessed | tf_op | source)
XLA Modules:
  0.0 77.0 jit_solution(540917321883923942)
XLA Ops:
  0.0 0.0 copy-start
  0.0 0.7 copy-done
  0.7 0.7 copy.45.refs_0_
  1.3 73.7 %shard_map.406 = f32[2,3,192,128]{3,2,1,0:T(8,128)} custom-call(f32[3,2]{1,0:T(4,128)} %copy.45.refs_0_, f32[2,3,192,128]{3,2,1,0:T(8,128)} %bitcast.5, f32[192,128]{1,0:T(8,128)} %bitcast.6, s32[192,128]{1,0:T(8,128)} %bitcast.7, bf16[240,32]{1,0:T(8,128)(2,1)} %constant.80.clone.refs_4_, bf16[2,32,512]{2,1,0:T(8,128)(2,1)} %constant.81.clone.refs_5_, ...), custom_call_target="tpu_custom_call" | custom-call | tf_op jit(solution)/shard_map/pallas_call | solution.py:994
  75.1 1.9 %copy.47 = f32[2,3,12,16,128]{4,3,2,1,0:T(8,128)} copy(f32[2,3,12,16,128]{4,3,2,1,0:T(8,128)} %bitcast.4) | data formatting | bytes 1179648
Async XLA Ops:
  0.0 0.7 copy-start

commit v3 on v2

--- a/solution.py
+++ b/solution.py
@@ -103,6 +103,7 @@
             self.kp = up(self.rows, 128)
             self.kb = 3 * self.kp
         self.packed = self.kb == 256
+        self.split = not self.packed and 0 < 3 * self.nb <= 256 == self.kp
         self.seg = 256 if self.packed else self.kp
 
     def row(self, x, y):
@@ -421,6 +422,8 @@
         clear(f"pend{l}")
     for l in range(len(levels)):
         clear(f"u{l}")
+        if levels[l].split:
+            clear(f"ub{l}")
 
     for one in moves[:first_moves]:
         one.wait()
@@ -473,9 +476,12 @@
     def copies(l, slot):
         for i, (dx, dy) in enumerate(DIRS):
             kind, at = ("d", i - 4) if dx and dy else ("x", i) if dx else ("y", i - 2)
+            src, dst = R[f"send{kind}{l}"].at[at], R[f"recv{kind}{l}"].at[slot, at]
+            if kind == "d":
+                src, dst = src.at[pl.ds(0, 3)], dst.at[pl.ds(0, 3)]
             yield dx, dy, pltpu.make_async_remote_copy(
-                src_ref=R[f"send{kind}{l}"].at[at],
-                dst_ref=R[f"recv{kind}{l}"].at[slot, at],
+                src_ref=src,
+                dst_ref=dst,
                 send_sem=R[f"ssem{l}"].at[i],
                 recv_sem=R[f"rsem{l}"].at[slot, i],
                 device_id=device(dx, dy),
@@ -487,21 +493,30 @@
         ys, run, nx = lev.ys, lev.run, lev.nx
         sx, sy, sd = (R[f"send{n}{l}"] for n in "xyd")
         tile = 3 * run
+        order = list(copies(l, slot))
+        lows, highs = [v[0:ys] for v in part], [v[ys : 2 * ys] for v in part]
         for c in range(3):
+            low, high = lows[c], highs[c]
             sx[0, c * run : (c + 1) * run] = part[c][lev.base : lev.base + run]
             sx[1, c * run : (c + 1) * run] = part[c][2 * ys : 2 * ys + run]
-            low, high = part[c][0:ys], part[c][ys : 2 * ys]
             sx[0, tile + c : tile + c + 1] = low[0:1]
             sx[0, tile + 3 + c : tile + 4 + c] = high[0:1]
             sx[1, tile + c : tile + c + 1] = low[nx : nx + 1]
             sx[1, tile + 3 + c : tile + 4 + c] = high[nx : nx + 1]
-            sy[0, c * ys : (c + 1) * ys] = low
-            sy[1, c * ys : (c + 1) * ys] = high
-            sd[0, 3 + c : 4 + c] = low[0:1]
+        for dx, dy, copy in order[0:2]:
+            pl.when(reach(dx, dy))(copy.start)
+        for c in range(3):
+            low, high = lows[c], highs[c]
+            sd[0, c : c + 1] = low[0:1]
             sd[1, c : c + 1] = high[0:1]
-            sd[2, 3 + c : 4 + c] = low[nx : nx + 1]
+            sd[2, c : c + 1] = low[nx : nx + 1]
             sd[3, c : c + 1] = high[nx : nx + 1]
-        for dx, dy, copy in copies(l, slot):
+        for dx, dy, copy in order[4:8]:
+            pl.when(reach(dx, dy))(copy.start)
+        for c in range(3):
+            sy[0, c * ys : (c + 1) * ys] = lows[c]
+            sy[1, c * ys : (c + 1) * ys] = highs[c]
+        for dx, dy, copy in order[2:4]:
             pl.when(reach(dx, dy))(copy.start)
 
     def arrive(l, slot):
@@ -512,16 +527,17 @@
             pl.when(reach(dx, dy))(copy.wait_send)
         rx, ry, rd = (R[f"recv{n}{l}"] for n in "xyd")
         tile = pl.ds(3 * run, 8)
-        left = rx[slot, 1, tile, :] + rd[slot, 2] + rd[slot, 3]
-        right = rx[slot, 0, tile, :] + rd[slot, 0] + rd[slot, 1]
+        left, right = rx[slot, 1, tile, :], rx[slot, 0, tile, :]
         at = lax.broadcasted_iota(jnp.int32, (ys, lev.lanes), 0)
         out = []
         for c in range(3):
             pieces = []
             for k, src in ((0, 1), (1, 0)):
                 val = ry[slot, src, c * ys : (c + 1) * ys, :]
-                val = val + jnp.where(at == 0, left[3 * k + c : 3 * k + c + 1], 0.0)
-                val = val + jnp.where(at == nx, right[3 * k + c : 3 * k + c + 1], 0.0)
+                row = slice(3 * k + c, 3 * k + c + 1)
+                low = left[row] + rd[slot, 3 - k, c : c + 1, :]
+                high = right[row] + rd[slot, 1 - k, c : c + 1, :]
+                val = val + jnp.where(at == 0, low, 0.0) + jnp.where(at == nx, high, 0.0)
                 pieces.append(val)
             pieces.append(rx[slot, 0, c * run : (c + 1) * run, :])
             pieces.append(rx[slot, 1, c * run : (c + 1) * run, :])
@@ -582,6 +598,11 @@
         R[f"u{l}"][at : at + b - a] = hi
         R[f"u{l}"][at + lev.kp : at + lev.kp + b - a] = hi
         R[f"u{l}"][at + 2 * lev.kp : at + 2 * lev.kp + b - a] = lo
+        if lev.split and a < lev.nb:
+            n = min(b, lev.nb) - a
+            for i, half in enumerate((hi, hi, lo)):
+                at = 256 * c + i * lev.nb + a
+                R[f"ub{l}"][at : at + n] = half[0:n]
 
     def span(l, blk):
         lev = levels[l]
@@ -607,25 +628,58 @@
             R[f"x{l}"][c, a:b] = first
             set_u(l, c, a, b, s * first)
 
+    def ahead(l):
+        lev = levels[l]
+        if lev.split:
+            for c in range(3):
+                u = R[f"u{l}"][c * lev.kb : (c + 1) * lev.kb]
+                R[f"pre{l}"][c] = mm(R[f"wi{l}"][c], u)
+
+    def plane_sums(l, blk, n):
+        lev = levels[l]
+        kb = lev.kb
+        if blk == "b" and lev.split:
+            q = [
+                R[f"pre{l}"][c] + mm(R[f"wb{l}"][c], R[f"ub{l}"][256 * c : 256 * (c + 1)])
+                for c in range(3)
+            ]
+            q = [[v[i * n : (i + 1) * n] for i in range(4)] for v in q]
+            both = [q[0][i] + q[1][i] for i in range(3)]
+            last, plain = q[2], [q[0][3], q[1][3], q[2][3]]
+        else:
+            u, w1, w2 = R[f"u{l}"], R[f"w1{blk}{l}"], R[f"w2{blk}{l}"]
+            both = mm(w1[...], u[0 : 2 * kb])
+            last = mm(w2[...], u[2 * kb : 3 * kb])
+            both = [both[i * n : (i + 1) * n] for i in range(3)]
+            last = [last[i * n : (i + 1) * n] for i in range(4)]
+            mass = w2[3 * n : 4 * n]
+            plain = [mm(mass, u[0:kb]), mm(mass, u[kb : 2 * kb]), last[3]]
+        stretch = (2.0 * MU_SHEAR + LAMBDA_BULK) / MU_SHEAR
+        plain[2] = stretch * plain[2]
+        return [both[0], both[1], last[2]], plain, [last[0], last[1]], [both[2]]
+
     def local_sums(l, blk):
         lev = levels[l]
         a, b = span(l, blk)
-        n, kb = b - a, lev.kb
-        u, w1, w2 = R[f"u{l}"], R[f"w1{blk}{l}"], R[f"w2{blk}{l}"]
-        both = mm(w1[...], u[0 : 2 * kb])
-        last = mm(w2[...], u[2 * kb : 3 * kb])
-        mass = w2[3 * n : 4 * n]
-        plain = [mm(mass, u[0:kb]), mm(mass, u[kb : 2 * kb]), last[3 * n : 4 * n]]
-        stretch = (2.0 * MU_SHEAR + LAMBDA_BULK) / MU_SHEAR
-        plain[2] = stretch * plain[2]
+        n = b - a
 
         def along(which, parts):
-            return mm(jnp.concatenate([wide3(v) for v in parts], axis=0), R[f"z{l}"][which])
-
-        zm = along(M_, [both[0:n], both[n : 2 * n], last[2 * n : 3 * n]])
-        zk = along(K_, plain)
-        zt = along(T_, [last[0:n], last[n : 2 * n]])
-        zg = along(G_, [both[2 * n : 3 * n]])
+            z = R[f"z{l}"]
+            if blk == "b" and lev.split:
+                pairs = [halves(v) for v in parts]
+                high = [v for v, _ in pairs]
+                tall = jnp.concatenate(high + [v for _, v in pairs], axis=0)
+                first = mm(tall, z[which, 0 : lev.lanes])
+                m = len(parts) * n
+                low = mm(jnp.concatenate(high, axis=0), z[which, 2 * lev.lanes : 3 * lev.lanes])
+                return first[0:m] + first[m : 2 * m] + low
+            return mm(jnp.concatenate([wide3(v) for v in parts], axis=0), z[which])
+
+        mass, stiff, trans, mixed = plane_sums(l, blk, n)
+        zm = along(M_, mass)
+        zk = along(K_, stiff)
+        zt = along(T_, trans)
+        zg = along(G_, mixed)
         return [
             zm[0:n] + zk[0:n] + zt[0:n],
             zm[n : 2 * n] + zk[n : 2 * n] + zt[n : 2 * n],
@@ -655,6 +709,7 @@
         send(l, slot, part)
         inner = local_sums(l, "i")
         advance(l, k, lev.nb, lev.rows, inner)
+        ahead(l)
         if beside is not None:
             beside()
         got = arrive(l, slot)
@@ -740,6 +795,7 @@
             R[f"d{l}"][c] = step
             R[f"x{l}"][c] += step
             set_u(l, c, 0, lev.rows, s * step)
+        ahead(l)
 
     def build(l):
         lev = levels[l]
@@ -775,7 +831,7 @@
 
         def store(kind, group, at, value):
             hi, lo = halves(value)
-            for blk in "bi" if lev.nb else "i":
+            for blk in "bi" if lev.nb and not lev.split else "i":
                 a, b = span(l, blk)
                 ref, row = R[f"{kind}{blk}{l}"], group * (b - a)
                 row = slice(row, row + b - a)
@@ -791,6 +847,21 @@
             store("w1", group, side * lev.kb, value)
         for group, value in enumerate(second):
             store("w2", group, 0, value)
+        if lev.split:
+            n, kp = lev.nb, lev.kp
+            lane = lax.broadcasted_iota(jnp.int32, (n, kp), 1)
+            parts = [(side, group, value) for group, side, value in first]
+            parts += [(2, group, value) for group, value in enumerate(second)]
+            parts += [(0, 3, second[3]), (1, 3, second[3])]
+            for side, group, value in parts:
+                hi, lo = (v.astype(F32) for v in halves(value[0:n]))
+                rows = slice(group * n, (group + 1) * n)
+                inner = [jnp.where(lane >= n, v, 0.0).astype(BF16) for v in (hi, lo)]
+                for i, half in enumerate((inner[0], inner[1], inner[0])):
+                    R[f"wi{l}"][side, rows, i * kp : (i + 1) * kp] = half
+                hi, lo = (jnp.where(lane < n, v, 0.0) for v in (hi, lo))
+                mixed = hi + pltpu.roll(lo, n, 1) + pltpu.roll(hi, 2 * n, 1)
+                R[f"wb{l}"][side, rows] = mixed.astype(BF16)
 
     build(0)
 
@@ -801,6 +872,7 @@
     clear_spare(top.nb, top.rows)
     prepare(0, top.nb, top.rows)
     begin(0, top.nb, top.rows, [R["r0"][c, top.nb : top.rows] for c in range(3)])
+    ahead(0)
     for dx, dy, copy in first_copies():
         pl.when(reach(dx, dy))(copy.wait_send)
         pl.when(reach(-dx, -dy))(copy.wait_recv)
@@ -862,21 +934,13 @@
         for x in range(nx):
             row = top.base + x * run
             R["x0"][c, row : row + 1, :] = R["x0"][c, x : x + 1, :]
-    backs = [
-        pltpu.make_async_copy(
-            R["x0"].at[:, body_rows, pl.ds(v * nz, nz)], R["out"].at[v], R["lsem"].at[v]
-        )
-        for v in range(vecs)
-    ]
-    for one in backs:
-        one.start()
-    for one in backs:
-        one.wait()
+    for v in range(vecs):
+        R["out"][v] = R["x0"][:, top.base : top.base + nx * run, v * nz : (v + 1) * nz]
 
 
 def chebyshev_table(spectrum, coef):
     for l in range(3):
-        low, top = spectrum[l, 0], spectrum[l, 1]
+        low, top = spectrum[0, l], spectrum[1, l]
         center = 0.5 * (top + low)
         radius = 0.5 * (top - low)
         ratio = center / radius
@@ -910,7 +974,7 @@
         levels.append(Level(*size) if step < DEGREES[0] else Wide(*size, COARSE_DEG - 1))
     top = levels[0]
     assert ny == top.run and nz % 128 == 0
-    add("spectrum_in", spectrum)
+    add("spectrum_in", spectrum.T)
     add("modes", modes.reshape(vecs, 3, nx * ny, nz))
     add("moduli_in", moduli.reshape(nx * ny, nz))
     add("pinned_in", pinned.reshape(nx * ny, nz))
@@ -963,9 +1027,14 @@
             temp(f"{n}{l}", pltpu.VMEM(field, F32))
         temp(f"u{l}", pltpu.VMEM((3 * lev.kb, lev.lanes), BF16))
         for blk, n in (("b", lev.nb), ("i", lev.rows - lev.nb)):
-            if n:
+            if n and not (blk == "b" and lev.split):
                 temp(f"w1{blk}{l}", pltpu.VMEM((3 * n, 2 * lev.kb), BF16))
                 temp(f"w2{blk}{l}", pltpu.VMEM((4 * n, lev.kb), BF16))
+        if lev.split:
+            temp(f"ub{l}", pltpu.VMEM((3 * 256, lev.lanes), BF16))
+            temp(f"pre{l}", pltpu.VMEM((3, 4 * lev.nb, lev.lanes), F32))
+            temp(f"wi{l}", pltpu.VMEM((3, 4 * lev.nb, lev.kb), BF16))
+            temp(f"wb{l}", pltpu.VMEM((3, 4 * lev.nb, 256), BF16))
         if lev is wide:
             continue
         for n in ("own", "pend"):
@@ -993,12 +1062,12 @@
     temp("frecv", pltpu.SemaphoreType.DMA((4,)))
     out = pl.pallas_call(
         functools.partial(kernel, levels, all_names),
-        out_shape=jax.ShapeDtypeStruct((vecs, 3, nx * ny, nz), F32),
+        out_shape=pltpu.VMEM((vecs, 3, nx * ny, nz), F32),
         in_specs=specs,
-        out_specs=pl.BlockSpec(memory_space=pl.ANY),
+        out_specs=pl.BlockSpec(memory_space=pltpu.VMEM),
         scratch_shapes=scratch,
         compiler_params=pltpu.CompilerParams(
-            collective_id=0, has_side_effects=True, vmem_limit_bytes=60 * 1024 * 1024
+            collective_id=0, has_side_effects=True, vmem_limit_bytes=62 * 1024 * 1024
         ),
     )(*args)
     return out.reshape(modes.shape)

time: 77.8 us -> 72.1 us (0.927)
  Pallas kernels: 73.7 us -> 70.4 us
  local copies, waits for them, and re-layouts: 3.28 us -> 0.82 us
    pallas_call x1, Pallas kernels: 73.7 us -> 70.4 us  [local(): pl.pallas_call(functools.partial(kernel, levels, all_names), out_shape=pl...]
    unnamed x4 -> x1, local copies, waits for them, and re-layouts: 3.28 us -> 0.82 us
where the time goes in v3:
time: 72.1 us; the launch traced here: 71.3 us
  Pallas kernels  70.4 us (98%)
  local copies, waits for them, and re-layouts  0.82 us (1%)
    pallas_call x1, Pallas kernels, local(): pl.pallas_call(functools.partial(kernel, levels, all_names), out_shape=pl...  70.4 us

profile of v3, /device:TPU:17, one launch (start us, length us, event | category | flops | bytes accessed | tf_op | source)
XLA Modules:
  0.0 71.3 jit_solution(2634612901388795151)
XLA Ops:
  0.0 70.4 %shard_map.406 = f32[2,3,192,128]{3,2,1,0:T(8,128)S(1)} custom-call(f32[2,3]{1,0:T(2,128)} %bitcast.9, f32[2,3,192,128]{3,2,1,0:T(8,128)} %bitcast.6, f32[192,128]{1,0:T(8,128)} %bitcast.7, s32[192,128]{1,0:T(8,128)} %bitcast.8, bf16[240,32]{1,0:T(8,128)(2,1)} %constant.80.clone.refs_4_, bf16[2,32,512]{2,1,0:T(8,128)(2,1)} %constant.81.clone.refs_5_, ...), custom_call_target="tpu_custom_call" | custom-call | tf_op jit(solution)/shard_map/pallas_call | solution.py:1063
  70.5 0.8 %copy.46 = f32[2,3,12,16,128]{4,3,2,1,0:T(8,128)} copy(f32[2,3,12,16,128]{4,3,2,1,0:T(8,128)S(1)} %bitcast.5) | data formatting | bytes 1179648

commit v4 on v3

--- a/solution.py
+++ b/solution.py
@@ -190,11 +190,17 @@
         self.lanes = up(vecs * nz, 128)
         self.half = self.lanes // 2
         assert vecs * nz <= self.half
-        self.where = {}
-        for x in range(-self.low, nx + self.low + 1):
-            for y in range(-self.low, ny + self.low + 1):
-                self.where[x, y] = len(self.where)
+        spots = [
+            (max(-x, x - nx, -y, y - ny, 0), x, y)
+            for x in range(-self.low, nx + self.low + 1)
+            for y in range(-self.low, ny + self.low + 1)
+        ]
+        self.where = {(x, y): row for row, (_, x, y) in enumerate(sorted(spots))}
         self.rows = up(len(self.where), 16)
+        self.needed = [
+            up(sum(away <= (ring - 1 - k) * degree for away, _, _ in spots), 16)
+            for k in range(ring)
+        ]
         self.nb = 0
         self.columns()
         self.plan()
@@ -488,43 +494,44 @@
                 device_id_type=pl.DeviceIdType.MESH,
             )
 
-    def send(l, slot, part):
+    def send(l, slot, part, only=range(8)):
         lev = levels[l]
         ys, run, nx = lev.ys, lev.run, lev.nx
         sx, sy, sd = (R[f"send{n}{l}"] for n in "xyd")
         tile = 3 * run
         order = list(copies(l, slot))
         lows, highs = [v[0:ys] for v in part], [v[ys : 2 * ys] for v in part]
-        for c in range(3):
-            low, high = lows[c], highs[c]
-            sx[0, c * run : (c + 1) * run] = part[c][lev.base : lev.base + run]
-            sx[1, c * run : (c + 1) * run] = part[c][2 * ys : 2 * ys + run]
-            sx[0, tile + c : tile + c + 1] = low[0:1]
-            sx[0, tile + 3 + c : tile + 4 + c] = high[0:1]
-            sx[1, tile + c : tile + c + 1] = low[nx : nx + 1]
-            sx[1, tile + 3 + c : tile + 4 + c] = high[nx : nx + 1]
-        for dx, dy, copy in order[0:2]:
-            pl.when(reach(dx, dy))(copy.start)
-        for c in range(3):
-            low, high = lows[c], highs[c]
-            sd[0, c : c + 1] = low[0:1]
-            sd[1, c : c + 1] = high[0:1]
-            sd[2, c : c + 1] = low[nx : nx + 1]
-            sd[3, c : c + 1] = high[nx : nx + 1]
-        for dx, dy, copy in order[4:8]:
-            pl.when(reach(dx, dy))(copy.start)
-        for c in range(3):
-            sy[0, c * ys : (c + 1) * ys] = lows[c]
-            sy[1, c * ys : (c + 1) * ys] = highs[c]
-        for dx, dy, copy in order[2:4]:
-            pl.when(reach(dx, dy))(copy.start)
-
-    def arrive(l, slot):
+        def launch(which):
+            for i in which:
+                if i in only:
+                    dx, dy, copy = order[i]
+                    pl.when(reach(dx, dy))(copy.start)
+
+        for i, start, at in ((0, lev.base, 0), (1, 2 * ys, nx)):
+            if i in only:
+                for c in range(3):
+                    sx[i, c * run : (c + 1) * run] = part[c][start : start + run]
+                    sx[i, tile + c : tile + c + 1] = lows[c][at : at + 1]
+                    sx[i, tile + 3 + c : tile + 4 + c] = highs[c][at : at + 1]
+        launch((0, 1))
+        for i, (src, at) in enumerate(((lows, 0), (highs, 0), (lows, nx), (highs, nx))):
+            if 4 + i in only:
+                for c in range(3):
+                    sd[i, c : c + 1] = src[c][at : at + 1]
+        launch((4, 5, 6, 7))
+        for i, src in enumerate((lows, highs)):
+            if 2 + i in only:
+                for c in range(3):
+                    sy[i, c * ys : (c + 1) * ys] = src[c]
+        launch((2, 3))
+
+    def arrive(l, slot, only=range(8)):
         lev = levels[l]
         ys, run, nx = lev.ys, lev.run, lev.nx
-        for dx, dy, copy in copies(l, slot):
-            pl.when(reach(-dx, -dy))(copy.wait_recv)
-            pl.when(reach(dx, dy))(copy.wait_send)
+        for i, (dx, dy, copy) in enumerate(copies(l, slot)):
+            if i in only:
+                pl.when(reach(-dx, -dy))(copy.wait_recv)
+                pl.when(reach(dx, dy))(copy.wait_send)
         rx, ry, rd = (R[f"recv{n}{l}"] for n in "xyd")
         tile = pl.ds(3 * run, 8)
         left, right = rx[slot, 1, tile, :], rx[slot, 0, tile, :]
@@ -635,7 +642,7 @@
                 u = R[f"u{l}"][c * lev.kb : (c + 1) * lev.kb]
                 R[f"pre{l}"][c] = mm(R[f"wi{l}"][c], u)
 
-    def plane_sums(l, blk, n):
+    def plane_sums(l, blk, n, step):
         lev = levels[l]
         kb = lev.kb
         if blk == "b" and lev.split:
@@ -648,20 +655,25 @@
             last, plain = q[2], [q[0][3], q[1][3], q[2][3]]
         else:
             u, w1, w2 = R[f"u{l}"], R[f"w1{blk}{l}"], R[f"w2{blk}{l}"]
-            both = mm(w1[...], u[0 : 2 * kb])
-            last = mm(w2[...], u[2 * kb : 3 * kb])
+            tall = [
+                w[...] if n == step
+                else jnp.concatenate([w[i * step : i * step + n] for i in range(g)], axis=0)
+                for w, g in ((w1, 3), (w2, 4))
+            ]
+            both = mm(tall[0], u[0 : 2 * kb])
+            last = mm(tall[1], u[2 * kb : 3 * kb])
             both = [both[i * n : (i + 1) * n] for i in range(3)]
             last = [last[i * n : (i + 1) * n] for i in range(4)]
-            mass = w2[3 * n : 4 * n]
+            mass = w2[3 * step : 3 * step + n]
             plain = [mm(mass, u[0:kb]), mm(mass, u[kb : 2 * kb]), last[3]]
         stretch = (2.0 * MU_SHEAR + LAMBDA_BULK) / MU_SHEAR
         plain[2] = stretch * plain[2]
         return [both[0], both[1], last[2]], plain, [last[0], last[1]], [both[2]]
 
-    def local_sums(l, blk):
+    def local_sums(l, blk, rows=None):
         lev = levels[l]
         a, b = span(l, blk)
-        n = b - a
+        n = rows or b - a
 
         def along(which, parts):
             z = R[f"z{l}"]
@@ -675,7 +687,7 @@
                 return first[0:m] + first[m : 2 * m] + low
             return mm(jnp.concatenate([wide3(v) for v in parts], axis=0), z[which])
 
-        mass, stiff, trans, mixed = plane_sums(l, blk, n)
+        mass, stiff, trans, mixed = plane_sums(l, blk, n, b - a)
         zm = along(M_, mass)
         zk = along(K_, stiff)
         zt = along(T_, trans)
@@ -714,6 +726,36 @@
             beside()
         got = arrive(l, slot)
         advance(l, k, 0, lev.nb, [own[c] + got[c] for c in range(3)])
+
+    def finish(k, slot):
+        only = [i for i, (dx, dy) in enumerate(DIRS) if dx >= 0 and dy >= 0]
+        c1, c2 = R["coef"][0, 2 * k], R["coef"][0, 2 * k + 1]
+
+        def result(c, a, b, sums):
+            s, f, d = R["s0"][a:b], R["f0"][a:b], R["d0"][c, a:b]
+            res = R["r0"][c, a:b] - (s * sums + f * d)
+            return R["x0"][c, a:b] + (c1 * d + c2 * (R["dinv0"][c, a:b] * res))
+
+        def put_out(c, start, value):
+            for v in range(vecs):
+                size = value.shape[0]
+                R["out"][v, c, start : start + size] = value[:, v * nz : (v + 1) * nz]
+
+        own = R["own0"]
+        part = local_sums(0, "b")
+        for c in range(3):
+            part[c] = part[c] + R["pend0"][c]
+            own[c] = part[c]
+        send(0, slot, part, only)
+        inner = local_sums(0, "i")
+        for c in range(3):
+            put_out(c, top.run, result(c, top.nb, top.rows, inner[c]))
+        got = arrive(0, slot, only)
+        for c in range(3):
+            value = result(c, 0, top.nb, own[c] + got[c])
+            put_out(c, 0, value[top.base : top.nb])
+            for x in range(top.nx):
+                put_out(c, x * top.run, value[x : x + 1])
 
     def restrict(l):
         lev = levels[l]
@@ -779,11 +821,8 @@
         right = [both, pltpu.roll(both, half, 1), one + pltpu.roll(two, half, 1)]
         begin(l, 0, n, [keep * v for v in right])
 
-        def body(k, _):
-            advance(l, k, 0, n, local_sums(l, "i"))
-            return 0
-
-        lax.fori_loop(0, COARSE_DEG - 1, body, 0)
+        for k, rows in enumerate(wide.needed):
+            advance(l, k, 0, rows, local_sums(l, "i", rows))
 
     def ascend(l):
         lev, n = levels[l], levels[l + 1].rows
@@ -927,15 +966,13 @@
             descend(l + 1, 0, restrict(l))
             cycle(l + 1)
         ascend(l)
-        lax.fori_loop(DEG, 2 * DEG, tail, 0)
+        if l:
+            lax.fori_loop(DEG, 2 * DEG, tail, 0)
+        else:
+            lax.fori_loop(DEG, 2 * DEG - 1, tail, 0)
+            finish(2 * DEG - 1, (2 * DEG + skip) % 2)
 
     cycle(0)
-    for c in range(3):
-        for x in range(nx):
-            row = top.base + x * run
-            R["x0"][c, row : row + 1, :] = R["x0"][c, x : x + 1, :]
-    for v in range(vecs):
-        R["out"][v] = R["x0"][:, top.base : top.base + nx * run, v * nz : (v + 1) * nz]
 
 
 def chebyshev_table(spectrum, coef):
@@ -973,7 +1010,7 @@
         size = (degree, nx // step, ny // step, nz // step, vecs)
         levels.append(Level(*size) if step < DEGREES[0] else Wide(*size, COARSE_DEG - 1))
     top = levels[0]
-    assert ny == top.run and nz % 128 == 0
+    assert ny == top.run and nz % 128 == 0 and top.rows == top.base + nx * ny
     add("spectrum_in", spectrum.T)
     add("modes", modes.reshape(vecs, 3, nx * ny, nz))
     add("moduli_in", moduli.reshape(nx * ny, nz))

time: 72.1 us -> 69.9 us (0.969)
  Pallas kernels: 70.4 us -> 69 us
    pallas_call x1, Pallas kernels: 70.4 us -> 69 us  [local(): pl.pallas_call(functools.partial(kernel, levels, all_names), out_shape=pl...]
where the time goes in v4:
time: 69.9 us; the launch traced here: 69.8 us
  Pallas kernels  69 us (99%)
  local copies, waits for them, and re-layouts  0.82 us (1%)
    pallas_call x1, Pallas kernels, local(): pl.pallas_call(functools.partial(kernel, levels, all_names), out_shape=pl...  69 us

profile of v4, /device:TPU:17, one launch (start us, length us, event | category | flops | bytes accessed | tf_op | source)
XLA Modules:
  0.0 69.8 jit_solution(10727608652396242708)
XLA Ops:
  0.0 69.0 %shard_map.406 = f32[2,3,192,128]{3,2,1,0:T(8,128)S(1)} custom-call(f32[2,3]{1,0:T(2,128)} %bitcast.9, f32[2,3,192,128]{3,2,1,0:T(8,128)} %bitcast.6, f32[192,128]{1,0:T(8,128)} %bitcast.7, s32[192,128]{1,0:T(8,128)} %bitcast.8, bf16[240,32]{1,0:T(8,128)(2,1)} %constant.80.clone.refs_4_, bf16[2,32,512]{2,1,0:T(8,128)(2,1)} %constant.81.clone.refs_5_, ...), custom_call_target="tpu_custom_call" | custom-call | tf_op jit(solution)/shard_map/pallas_call | solution.py:1100
  69.0 0.8 %copy.46 = f32[2,3,12,16,128]{4,3,2,1,0:T(8,128)} copy(f32[2,3,12,16,128]{4,3,2,1,0:T(8,128)S(1)} %bitcast.5) | data formatting | bytes 1179648

commit v5 on v4

--- a/solution.py
+++ b/solution.py
@@ -219,8 +219,6 @@
                 nodes = tuple(
                     (x, y) for x, y in closed if (x - dx * nx, y - dy * ny) in self.where
                 )
-                if abs(dx) <= 1 and abs(dy) <= 1:
-                    nodes = tuple(closed)
                 if not nodes:
                     continue
                 if nodes not in kinds:
@@ -379,6 +377,29 @@
     for v in range(vecs):
         load(R["modes"].at[v], R["r0"].at[:, body_rows, pl.ds(v * nz, nz)])
     first_moves = len(moves)
+    wide = levels[-1]
+    edged = range(len(levels) - 1)
+
+    def clear(name):
+        R[name][...] = jnp.zeros_like(R[name])
+
+    for l in edged:
+        for n in "xyd":
+            clear(f"recv{n}{l}")
+    for n in ("gotx", "goty", "gotd", "gets", "getb"):
+        clear(n)
+
+    barrier = pltpu.get_barrier_semaphore()
+    peers = [(dx, dy) for dx, dy, *_ in wide.sends if dx or dy]
+    assert set(DIRS) <= set(peers)
+    for dx, dy in peers:
+
+        @pl.when(reach(dx, dy))
+        def _():
+            pl.semaphore_signal(
+                barrier, inc=1, device_id=device(dx, dy), device_id_type=pl.DeviceIdType.MESH
+            )
+
     for l, lev in enumerate(levels):
         if lev.nz % 128 == 0:
             R[f"z{l}"][...] = jnp.zeros_like(R[f"z{l}"])
@@ -398,29 +419,6 @@
                         )
             else:
                 load(R[name], R[name[:-3]])
-
-    wide = levels[-1]
-    edged = range(len(levels) - 1)
-
-    def clear(name):
-        R[name][...] = jnp.zeros_like(R[name])
-
-    for l in edged:
-        for n in "xyd":
-            clear(f"recv{n}{l}")
-    for n in ("gotx", "goty", "gotd", "gets", "getb"):
-        clear(n)
-
-    barrier = pltpu.get_barrier_semaphore()
-    peers = [(dx, dy) for dx, dy, *_ in wide.sends if dx or dy]
-    assert set(DIRS) <= set(peers)
-    for dx, dy in peers:
-
-        @pl.when(reach(dx, dy))
-        def _():
-            pl.semaphore_signal(
-                barrier, inc=1, device_id=device(dx, dy), device_id_type=pl.DeviceIdType.MESH
-            )
 
     for l in edged:
         for n in "xyd":
@@ -479,13 +477,14 @@
     for one in moves[first_moves:]:
         one.wait()
 
-    def copies(l, slot):
-        for i, (dx, dy) in enumerate(DIRS):
+    def copies(l, slot, only):
+        for i in only:
+            dx, dy = DIRS[i]
             kind, at = ("d", i - 4) if dx and dy else ("x", i) if dx else ("y", i - 2)
             src, dst = R[f"send{kind}{l}"].at[at], R[f"recv{kind}{l}"].at[slot, at]
             if kind == "d":
                 src, dst = src.at[pl.ds(0, 3)], dst.at[pl.ds(0, 3)]
-            yield dx, dy, pltpu.make_async_remote_copy(
+            yield i, dx, dy, pltpu.make_async_remote_copy(
                 src_ref=src,
                 dst_ref=dst,
                 send_sem=R[f"ssem{l}"].at[i],
@@ -499,7 +498,7 @@
         ys, run, nx = lev.ys, lev.run, lev.nx
         sx, sy, sd = (R[f"send{n}{l}"] for n in "xyd")
         tile = 3 * run
-        order = list(copies(l, slot))
+        order = {i: rest for i, *rest in copies(l, slot, only)}
         lows, highs = [v[0:ys] for v in part], [v[ys : 2 * ys] for v in part]
         def launch(which):
             for i in which:
@@ -528,10 +527,8 @@
     def arrive(l, slot, only=range(8)):
         lev = levels[l]
         ys, run, nx = lev.ys, lev.run, lev.nx
-        for i, (dx, dy, copy) in enumerate(copies(l, slot)):
-            if i in only:
-                pl.when(reach(-dx, -dy))(copy.wait_recv)
-                pl.when(reach(dx, dy))(copy.wait_send)
+        for _, dx, dy, copy in copies(l, slot, only):
+            pl.when(reach(-dx, -dy))(copy.wait_recv)
         rx, ry, rd = (R[f"recv{n}{l}"] for n in "xyd")
         tile = pl.ds(3 * run, 8)
         left, right = rx[slot, 1, tile, :], rx[slot, 0, tile, :]
@@ -551,6 +548,10 @@
             out.append(jnp.concatenate(pieces, axis=0))
         return out
 
+    def settle(l, slot, only=range(8)):
+        for _, dx, dy, copy in copies(l, slot, only):
+            pl.when(reach(dx, dy))(copy.wait_send)
+
     def wide_copies(kind):
         index = 0
         for dx, dy, start, size, at, nodes in wide.sends:
@@ -642,7 +643,19 @@
                 u = R[f"u{l}"][c * lev.kb : (c + 1) * lev.kb]
                 R[f"pre{l}"][c] = mm(R[f"wi{l}"][c], u)
 
-    def plane_sums(l, blk, n, step):
+    def ahead_inner():
+        n = top.rows - top.nb
+        u = R["u0"]
+        for at in range(0, 3 * top.kb, top.kp):
+            u[at : at + top.nb] = jnp.zeros((top.nb, top.lanes), BF16)
+        w1, w2, kb = R["w1i0"], R["w2i0"], top.kb
+        R["inner"][0 : 3 * n] = mm(w1[...], u[0 : 2 * kb])
+        R["inner"][3 * n : 7 * n] = mm(w2[...], u[2 * kb : 3 * kb])
+        for c in range(2):
+            at = (7 + c) * n
+            R["inner"][at : at + n] = mm(w2[3 * n : 4 * n], u[c * kb : (c + 1) * kb])
+
+    def plane_sums(l, blk, n, step, early):
         lev = levels[l]
         kb = lev.kb
         if blk == "b" and lev.split:
@@ -653,6 +666,13 @@
             q = [[v[i * n : (i + 1) * n] for i in range(4)] for v in q]
             both = [q[0][i] + q[1][i] for i in range(3)]
             last, plain = q[2], [q[0][3], q[1][3], q[2][3]]
+        elif early and lev.split:
+            q = [mm(R[f"wj{l}"][c], R[f"ub{l}"][256 * c : 256 * (c + 1)]) for c in range(3)]
+            q = [[v[i * n : (i + 1) * n] for i in range(4)] for v in q]
+            done = [R["inner"][i * n : (i + 1) * n] for i in range(9)]
+            both = [done[i] + q[0][i] + q[1][i] for i in range(3)]
+            last = [done[3 + i] + q[2][i] for i in range(4)]
+            plain = [done[7] + q[0][3], done[8] + q[1][3], last[3]]
         else:
             u, w1, w2 = R[f"u{l}"], R[f"w1{blk}{l}"], R[f"w2{blk}{l}"]
             tall = [
@@ -670,7 +690,7 @@
         plain[2] = stretch * plain[2]
         return [both[0], both[1], last[2]], plain, [last[0], last[1]], [both[2]]
 
-    def local_sums(l, blk, rows=None):
+    def local_sums(l, blk, rows=None, early=False):
         lev = levels[l]
         a, b = span(l, blk)
         n = rows or b - a
@@ -687,7 +707,7 @@
                 return first[0:m] + first[m : 2 * m] + low
             return mm(jnp.concatenate([wide3(v) for v in parts], axis=0), z[which])
 
-        mass, stiff, trans, mixed = plane_sums(l, blk, n, b - a)
+        mass, stiff, trans, mixed = plane_sums(l, blk, n, b - a, early)
         zm = along(M_, mass)
         zk = along(K_, stiff)
         zt = along(T_, trans)
@@ -726,6 +746,7 @@
             beside()
         got = arrive(l, slot)
         advance(l, k, 0, lev.nb, [own[c] + got[c] for c in range(3)])
+        settle(l, slot)
 
     def finish(k, slot):
         only = [i for i, (dx, dy) in enumerate(DIRS) if dx >= 0 and dy >= 0]
@@ -756,13 +777,14 @@
             put_out(c, 0, value[top.base : top.nb])
             for x in range(top.nx):
                 put_out(c, x * top.run, value[x : x + 1])
+        settle(0, slot, only)
 
     def restrict(l):
         lev = levels[l]
         masked = []
         for blk in "bi":
             a, b = span(l, blk)
-            sums = local_sums(l, blk)
+            sums = local_sums(l, blk, early=True)
             s, f = R[f"s{l}"][a:b], R[f"f{l}"][a:b]
             free = 1.0 - f
             if blk == "b":
@@ -808,6 +830,7 @@
         got = arrive(l, slot)
         free = 1.0 - R[f"f{l}"][0 : lev.nb]
         begin(l, 0, lev.nb, [free * (own[c] + got[c]) for c in range(3)])
+        settle(l, slot)
 
     def solve_wide(packed):
         l, n, half = len(levels) - 1, wide.rows, wide.half
@@ -888,19 +911,22 @@
             store("w2", group, 0, value)
         if lev.split:
             n, kp = lev.nb, lev.kp
-            lane = lax.broadcasted_iota(jnp.int32, (n, kp), 1)
+            lane = lax.broadcasted_iota(jnp.int32, (lev.rows, kp), 1)
             parts = [(side, group, value) for group, side, value in first]
             parts += [(2, group, value) for group, value in enumerate(second)]
             parts += [(0, 3, second[3]), (1, 3, second[3])]
             for side, group, value in parts:
-                hi, lo = (v.astype(F32) for v in halves(value[0:n]))
+                hi, lo = (v.astype(F32) for v in halves(value))
                 rows = slice(group * n, (group + 1) * n)
-                inner = [jnp.where(lane >= n, v, 0.0).astype(BF16) for v in (hi, lo)]
+                inner = [jnp.where(lane[0:n] >= n, v[0:n], 0.0).astype(BF16) for v in (hi, lo)]
                 for i, half in enumerate((inner[0], inner[1], inner[0])):
                     R[f"wi{l}"][side, rows, i * kp : (i + 1) * kp] = half
                 hi, lo = (jnp.where(lane < n, v, 0.0) for v in (hi, lo))
                 mixed = hi + pltpu.roll(lo, n, 1) + pltpu.roll(hi, 2 * n, 1)
-                R[f"wb{l}"][side, rows] = mixed.astype(BF16)
+                mixed = mixed.astype(BF16)
+                R[f"wb{l}"][side, rows] = mixed[0:n]
+                rest = lev.rows - n
+                R[f"wj{l}"][side, group * rest : (group + 1) * rest] = mixed[n : lev.rows]
 
     build(0)
 
@@ -943,7 +969,11 @@
             build(l)
 
     def pre(k, _):
-        smooth(0, k, k % 2, lambda: pl.when(k == 0)(coarse_setup))
+        def beside():
+            pl.when(k == 0)(coarse_setup)
+            pl.when(k == DEG - 2)(ahead_inner)
+
+        smooth(0, k, k % 2, beside)
         return 0
 
     def cycle(l):
@@ -1072,6 +1102,9 @@
             temp(f"pre{l}", pltpu.VMEM((3, 4 * lev.nb, lev.lanes), F32))
             temp(f"wi{l}", pltpu.VMEM((3, 4 * lev.nb, lev.kb), BF16))
             temp(f"wb{l}", pltpu.VMEM((3, 4 * lev.nb, 256), BF16))
+            rest = lev.rows - lev.nb
+            temp(f"wj{l}", pltpu.VMEM((3, 4 * rest, 256), BF16))
+            temp("inner", pltpu.VMEM((9 * rest, lev.lanes), F32))
         if lev is wide:
             continue
         for n in ("own", "pend"):

time: 69.9 us -> 68.7 us (0.983)
  Pallas kernels: 69 us -> 67.7 us
    pallas_call x1, Pallas kernels: 69 us -> 67.7 us  [local(): pl.pallas_call(functools.partial(kernel, levels, all_names), out_shape=pl...]
where the time goes in v5:
time: 68.7 us; the launch traced here: 68.6 us
  Pallas kernels  67.7 us (99%)
  local copies, waits for them, and re-layouts  0.82 us (1%)
    pallas_call x1, Pallas kernels, local(): pl.pallas_call(functools.partial(kernel, levels, all_names), out_shape=pl...  67.7 us

profile of v5, /device:TPU:17, one launch (start us, length us, event | category | flops | bytes accessed | tf_op | source)
XLA Modules:
  0.0 68.6 jit_solution(17933302993279504113)
XLA Ops:
  0.0 67.7 %shard_map.406 = f32[2,3,192,128]{3,2,1,0:T(8,128)S(1)} custom-call(f32[2,3]{1,0:T(2,128)} %bitcast.9, f32[2,3,192,128]{3,2,1,0:T(8,128)} %bitcast.6, f32[192,128]{1,0:T(8,128)} %bitcast.7, s32[192,128]{1,0:T(8,128)} %bitcast.8, bf16[240,32]{1,0:T(8,128)(2,1)} %constant.80.clone.refs_4_, bf16[2,32,512]{2,1,0:T(8,128)(2,1)} %constant.81.clone.refs_5_, ...), custom_call_target="tpu_custom_call" | custom-call | tf_op jit(solution)/shard_map/pallas_call | solution.py:1133
  67.7 0.8 %copy.46 = f32[2,3,12,16,128]{4,3,2,1,0:T(8,128)} copy(f32[2,3,12,16,128]{4,3,2,1,0:T(8,128)S(1)} %bitcast.5) | data formatting | bytes 1179648

commit v6 on v5

--- a/solution.py
+++ b/solution.py
@@ -214,22 +214,24 @@
         self.pack_rows = 0
         at = 0
         kinds = {}
-        for dx in range(-far[0], far[0] + 1):
-            for dy in range(-far[1], far[1] + 1):
-                nodes = tuple(
-                    (x, y) for x, y in closed if (x - dx * nx, y - dy * ny) in self.where
-                )
-                if not nodes:
-                    continue
-                if nodes not in kinds:
-                    k = len(nodes)
-                    size = up(k + -(-k // 2), 8)
-                    kinds[nodes] = (self.pack_rows, size)
-                    self.sections.append((self.pack_rows, size, nodes))
-                    self.pack_rows += size
-                start, size = kinds[nodes]
-                self.sends.append((dx, dy, start, size, at, nodes))
-                at += size
+        offsets = [
+            (dx, dy) for dx in range(-far[0], far[0] + 1) for dy in range(-far[1], far[1] + 1)
+        ]
+        for dx, dy in sorted(offsets, key=lambda o: (abs(o[0]) != 1, abs(o[1]), o)):
+            nodes = tuple(
+                (x, y) for x, y in closed if (x - dx * nx, y - dy * ny) in self.where
+            )
+            if not nodes:
+                continue
+            if nodes not in kinds:
+                k = len(nodes)
+                size = up(k + -(-k // 2), 8)
+                kinds[nodes] = (self.pack_rows, size)
+                self.sections.append((self.pack_rows, size, nodes))
+                self.pack_rows += size
+            start, size = kinds[nodes]
+            self.sends.append((dx, dy, start, size, at, nodes))
+            at += size
         self.pack_rows = up(self.pack_rows, 16)
         self.got_rows = up(at, 16)
 
@@ -454,9 +456,9 @@
     def first_copies():
         plan = (
             (-1, 0, R["r0"].at[:, edge, :], R["gotx"].at[pl.ds(0, 3)]),
-            (-1, 0, s0.at[edge, :], R["gotx"].at[3]),
+            (-1, 0, s0.at[edge, pl.ds(0, nz)], R["gotx"].at[3, :, pl.ds(0, nz)]),
             (0, -1, put, R["goty"]),
-            (-1, -1, R["putd"], R["gotd"]),
+            (-1, -1, R["putd"].at[pl.ds(0, 4)], R["gotd"].at[pl.ds(0, 4)]),
         )
         for i, (dx, dy, src, dst) in enumerate(plan):
             yield dx, dy, pltpu.make_async_remote_copy(
@@ -570,15 +572,18 @@
 
     def wide_send(kind, value):
         R[f"pack{kind}"][...] = value
+        for dx, dy, copy in wide_copies(kind):
+            pl.when(reach(dx, dy))(copy.start)
         for dx, dy, start, size, at, nodes in wide.sends:
             if dx == 0 and dy == 0:
                 R[f"get{kind}"][at : at + size] = value[start : start + size]
-        for dx, dy, copy in wide_copies(kind):
-            pl.when(reach(dx, dy))(copy.start)
 
     def wide_wait(kind):
         for dx, dy, copy in wide_copies(kind):
             pl.when(reach(-dx, -dy))(copy.wait_recv)
+
+    def wide_settle(kind):
+        for dx, dy, copy in wide_copies(kind):
             pl.when(reach(dx, dy))(copy.wait_send)
 
     def thirds(value):
@@ -595,6 +600,7 @@
 
     def wide_scale_take():
         wide_wait("s")
+        wide_settle("s")
         place = R["place"][0 : wide.rows]
         R[f"s{len(levels) - 1}"][...] = sum(mm(place, part) for part in thirds(R["gets"][...]))
         prepare(len(levels) - 1, 0, wide.rows)
@@ -843,6 +849,7 @@
         both, one, two = (spread[i * n : (i + 1) * n] for i in range(3))
         right = [both, pltpu.roll(both, half, 1), one + pltpu.roll(two, half, 1)]
         begin(l, 0, n, [keep * v for v in right])
+        wide_settle("b")
 
         for k, rows in enumerate(wide.needed):
             advance(l, k, 0, rows, local_sums(l, "i", rows))
@@ -942,6 +949,8 @@
         pl.when(reach(dx, dy))(copy.wait_send)
         pl.when(reach(-dx, -dy))(copy.wait_recv)
     clear_spare(top.base, top.nb)
+    for v in range(1, vecs):
+        R["gotx"][3, :, v * nz : (v + 1) * nz] = R["gotx"][3, :, 0:nz]
     ys, run, nx = top.ys, top.run, top.nx
     at = lax.broadcasted_iota(jnp.int32, (ys, top.lanes), 0)
     for c in range(4):

time: 68.7 us -> 68.7 us (level)
  no operation moved by 1% of the time
where the time goes in v6:
time: 68.7 us; the launch traced here: 68.6 us
  Pallas kernels  67.7 us (99%)
  local copies, waits for them, and re-layouts  0.82 us (1%)
    pallas_call x1, Pallas kernels, local(): pl.pallas_call(functools.partial(kernel, levels, all_names), out_shape=pl...  67.7 us

profile of v6, /device:TPU:17, one launch (start us, length us, event | category | flops | bytes accessed | tf_op | source)
XLA Modules:
  0.0 68.6 jit_solution(3345671151868436224)
XLA Ops:
  0.0 67.7 %shard_map.406 = f32[2,3,192,128]{3,2,1,0:T(8,128)S(1)} custom-call(f32[2,3]{1,0:T(2,128)} %bitcast.9, f32[2,3,192,128]{3,2,1,0:T(8,128)} %bitcast.6, f32[192,128]{1,0:T(8,128)} %bitcast.7, s32[192,128]{1,0:T(8,128)} %bitcast.8, bf16[240,32]{1,0:T(8,128)(2,1)} %constant.80.clone.refs_4_, bf16[2,32,512]{2,1,0:T(8,128)(2,1)} %constant.81.clone.refs_5_, ...), custom_call_target="tpu_custom_call" | custom-call | tf_op jit(solution)/shard_map/pallas_call | solution.py:1142
  67.7 0.8 %copy.46 = f32[2,3,12,16,128]{4,3,2,1,0:T(8,128)} copy(f32[2,3,12,16,128]{4,3,2,1,0:T(8,128)S(1)} %bitcast.5) | data formatting | bytes 1179648
